TPU v7x, 8 devices: a whole 2x2x1 slice. The times are simulated.
8 devices in a mesh: dp: 1 (over z), hp: 2 (over y), cp: 4 (over x, core).
Axes of the slice: x: 2, y: 2, z: 1, core: 2. Of those that a mesh axis runs over, the one named last changes fastest.
Arguments:
- latent: bfloat16 [48, 2, 128, 512], P(('dp', 'cp'), 'hp')
- conv_w: bfloat16 [4, 3, 3, 3, 512, 512], replicated
- conv_b: float32 [4, 512], replicated
- gn_gamma: float32 [4, 512], replicated
- gn_beta: float32 [4, 512], replicated
Outputs:
- output: bfloat16 [48, 2, 128, 512], P(('dp', 'cp'), 'hp')
All inputs are finite; a program needn't handle non-finite values.
Results may differ from a plain program's by a relative error of at most 0.00887298.
Values are sent between devices in bfloat16 or wider.
A program may use at most 1 GiB of HBM per device.

v0:
```python
import jax
import jax.numpy as jnp
from jax import lax
from jax.sharding import PartitionSpec as P

GROUPS = 32
EPS = 1e-6


def norm_silu(local_act, gamma, beta, total_count):
    frames, row_count, lat_width, channels = local_act.shape
    per_group = channels // GROUPS
    grouped = local_act.reshape(frames, row_count, lat_width, GROUPS, per_group).astype(jnp.float32)
    stat_sums = jnp.stack([jnp.sum(grouped, axis=(0, 1, 2, 4)), jnp.sum(grouped * grouped, axis=(0, 1, 2, 4))])
    stat_sums = lax.psum(stat_sums, ("cp", "hp"))
    mean_val = stat_sums[0] / total_count
    variance = stat_sums[1] / total_count - mean_val * mean_val
    inv_std = lax.rsqrt(variance + EPS)
    gamma_g = gamma.reshape(GROUPS, per_group)
    scale_c = (inv_std[:, None] * gamma_g).reshape(channels)
    shift_c = (beta.reshape(GROUPS, per_group) - (mean_val * inv_std)[:, None] * gamma_g).reshape(channels)
    return jax.nn.silu(local_act.astype(jnp.float32) * scale_c + shift_c).astype(jnp.bfloat16)


def conv_valid(padded, kernel, bias_vec):
    conv_out = lax.conv_general_dilated(padded[None], kernel, (1, 1, 1), ((0, 0), (0, 0), (1, 1)), dimension_numbers=("NDHWC", "DHWIO", "NDHWC"), preferred_element_type=jnp.float32)
    return (conv_out[0] + bias_vec).astype(jnp.bfloat16)


def solution(mesh):
    n_time = mesh.shape["cp"]
    n_rows = mesh.shape["hp"]
    time_fwd = [(i, i + 1) for i in range(n_time - 1)]
    rows_down = [(i, i + 1) for i in range(n_rows - 1)]
    rows_up = [(i + 1, i) for i in range(n_rows - 1)]

    def local_decode(local_lat, conv_w, conv_b, gn_gamma, gn_beta):
        frames, row_count, lat_width, channels = local_lat.shape
        total_count = frames * n_time * row_count * n_rows * lat_width * (channels // GROUPS)
        time_rank = lax.axis_index("cp")
        residual = local_lat
        for block_idx in range(2):
            hidden = residual
            for sub_idx in range(2):
                layer_idx = 2 * block_idx + sub_idx
                activated = norm_silu(hidden, gn_gamma[layer_idx], gn_beta[layer_idx], total_count)
                prev_frames = lax.ppermute(activated[frames - 2:], "cp", time_fwd)
                own_first = jnp.broadcast_to(activated[:1], prev_frames.shape)
                prev_frames = jnp.where(time_rank == 0, own_first, prev_frames)
                extended = jnp.concatenate([prev_frames, activated], axis=0)
                from_above = lax.ppermute(extended[:, row_count - 1:], "hp", rows_down)
                from_below = lax.ppermute(extended[:, :1], "hp", rows_up)
                extended = jnp.concatenate([from_above, extended, from_below], axis=1)
                hidden = conv_valid(extended, conv_w[layer_idx], conv_b[layer_idx])
            residual = (residual.astype(jnp.float32) + hidden.astype(jnp.float32)).astype(jnp.bfloat16)
        return residual

    video_spec = P(("dp", "cp"), "hp", None, None)
    return jax.shard_map(local_decode, mesh=mesh, in_specs=(video_spec, P(), P(), P(), P()), out_specs=video_spec, check_vma=False)
```

profile of v0, /device:TPU:0, one launch (start us, length us, event | category | flops | bytes accessed | tf_op | source)
XLA Modules:
  0.0 807.8 jit_solution(1070219251363420794)
XLA Ops:
  0.0 6.4 fusion.93
  9.7 25.1 %psum.28 = f32[2,32]{1,0:T(2,128)S(1)} all-reduce(f32[2,32]{1,0:T(2,128)S(1)} %pad_maximum_fusion.4), channel_id=1, replica_groups=mesh['dp'=1,'hp'=2,'cp'=4] {'cp','hp'}, use_global_device_ids=true, to_apply=%region_4.5 | all-reduce | flops 64 | bytes 512 | tf_op jit(solution)/shard_map/psum | solution.py:15
  35.1 8.5 %fusion.71 = bf16[12,1,128,512]{3,1,2,0:T(2,128)(2,1)S(1)} fusion(f32[512]{0:T(512)S(1)} %get-tuple-element.41, f32[512]{0:T(512)S(1)} %get-tuple-element.40, bf16[12,1,128,512]{3,2,1,0:T(8,128)(2,1)} %param.5), kind=kLoop, calls=%fused_computation.93 | loop fusion | flops 6291456 | bytes 3149824 | tf_op jit(solution)/shard_map/convert_element_type | solution.py:22
  54.4 5.3 collective-permute-start.1
  60.3 69.3 %collective-permute-done.2 = bf16[14,1,128,512]{3,1,2,0:T(2,128)(2,1)S(1)} collective-permute-done((bf16[14,1,128,512]{3,1,2,0:T(2,128)(2,1)S(1)}, bf16[14,1,128,512]{3,1,2,0:T(2,128)(2,1)S(1)}, u32[]{:S(2)}, u32[]{:S(2)}) %collective-permute-start.2) | collective-permute-done | bytes 1835040 | tf_op jit(solution)/shard_map/ppermute | solution.py:52
  131.5 20.0 %maximum_bitcast_fusion = bf16[14,3,1,128,512]{4,1,3,0,2:T(4,128)(2,1)} fusion(bf16[14,1,128,512]{3,1,2,0:T(2,128)(2,1)S(1)} %collective-permute-done.2, bf16[12,1,128,512]{3,1,2,0:T(2,128)(2,1)S(1)} %fusion.71, bf16[2,1,128,512]{3,1,2,0:T(2,128)(2,1)S(1)} %broadcast_select_fusion.3, bf16[14,1,128,512]{3,1,2,0:T(2,128)(2,1)S(1)} %collective-permute-done.1), kind=kLoop, calls=%fused_computation.17 | loop fusion | flops 22020096 | bytes 11010048 | tf_op jit(solution)/shard_map/broadcast_in_dim | solution.py:26
  151.5 10.0 %pad = bf16[14,3,1,136,512]{4,1,3,0,2:T(4,128)(2,1)} pad(bf16[14,3,1,128,512]{4,1,3,0,2:T(4,128)(2,1)} %maximum_bitcast_fusion, bf16[]{:T(256)} %constant.27), padding=0_0x0_0x0_0x1_7x0_0 | pad | bytes 11354114 | tf_op jit(solution)/shard_map/broadcast_in_dim | solution.py:26
  166.5 30.6 %fusion.40 = (f32[512]{0:T(512)S(1)}, f32[512]{0:T(512)S(1)}, f32[12,1,8,17,512]{4,2,3,1,0:T(8,128)}) fusion(pred[8,17]{0,1:T(8,128)(4,1)S(1)} %copy-done.6, f32[512]{0:T(512)S(1)} %bitcast.231, bf16[4,3,3,3,512,512]{5,4,3,2,1,0:T(8,128)(2,1)} %param.6, bf16[14,3,1,7,2,512]{5,3,4,1,0,2:T(8,128)(2,1)S(1)} %slice.138, ...), kind=kOutput, calls=%fused_computation.49 | convolution fusion | flops 23129358336 | bytes 23955592 | tf_op jit(solution)/shard_map/conv_general_dilated | solution.py:26
  197.5 33.3 %psum.29 = f32[2,32]{1,0:T(2,128)S(1)} all-reduce(f32[2,32]{1,0:T(2,128)S(1)} %pad_maximum_fusion.5), channel_id=1, replica_groups=mesh['dp'=1,'hp'=2,'cp'=4] {'cp','hp'}, use_global_device_ids=true, to_apply=%region_9.10 | all-reduce | flops 64 | bytes 512 | tf_op jit(solution)/shard_map/psum | solution.py:15
  231.1 5.4 copy.10
  236.5 7.5 fusion.70
  254.1 5.2 collective-permute-start.4
  259.3 71.0 %collective-permute-done.5 = bf16[14,1,128,512]{3,1,2,0:T(2,128)(2,1)S(1)} collective-permute-done((bf16[14,1,128,512]{3,1,2,0:T(2,128)(2,1)S(1)}, bf16[14,1,128,512]{3,1,2,0:T(2,128)(2,1)S(1)}, u32[]{:S(2)}, u32[]{:S(2)}) %collective-permute-start.5) | collective-permute-done | bytes 1835040 | tf_op jit(solution)/shard_map/ppermute | solution.py:52
  332.2 20.0 %maximum_bitcast_fusion.1 = bf16[14,3,1,128,512]{4,1,3,0,2:T(4,128)(2,1)} fusion(bf16[14,1,128,512]{3,1,2,0:T(2,128)(2,1)S(1)} %collective-permute-done.5, bf16[12,1,128,512]{3,1,2,0:T(2,128)(2,1)S(1)} %fusion.70, bf16[2,1,128,512]{3,1,2,0:T(2,128)(2,1)S(1)} %broadcast_select_fusion.2, bf16[14,1,128,512]{3,1,2,0:T(2,128)(2,1)S(1)} %collective-permute-done.4), kind=kLoop, calls=%fused_computation.18 | loop fusion | flops 22020096 | bytes 11010048 | tf_op jit(solution)/shard_map/broadcast_in_dim | solution.py:26
  352.2 10.0 %pad.2 = bf16[14,3,1,136,512]{4,1,3,0,2:T(4,128)(2,1)} pad(bf16[14,3,1,128,512]{4,1,3,0,2:T(4,128)(2,1)} %maximum_bitcast_fusion.1, bf16[]{:T(256)} %constant.27), padding=0_0x0_0x0_0x1_7x0_0 | pad | bytes 11354114 | tf_op jit(solution)/shard_map/broadcast_in_dim | solution.py:26
  367.2 28.3 %fusion.78 = f32[12,1,8,17,512]{4,2,3,1,0:T(8,128)S(1)} fusion(bf16[4,3,3,3,512,512]{5,4,3,2,1,0:T(8,128)(2,1)} %param.6, bf16[14,3,1,7,2,512]{5,3,4,1,0,2:T(8,128)(2,1)S(1)} %slice.142, bf16[14,3,1,8,17,512]{5,3,4,1,0,2:T(8,128)(2,1)S(1)} %copy.13, pred[8,17]{0,1:T(8,128)(4,1)S(1)} %copy-done.6), kind=kOutput, calls=%fused_computation.97 | convolution fusion | flops 23122673664 | bytes 23949448 | tf_op jit(solution)/shard_map/conv_general_dilated | solution.py:26
  399.0 7.1 convert_reduce_fusion
  406.5 31.1 %psum.30 = f32[2,32]{1,0:T(2,128)S(1)} all-reduce(f32[2,32]{1,0:T(2,128)S(1)} %pad_maximum_fusion.6), channel_id=1, replica_groups=mesh['dp'=1,'hp'=2,'cp'=4] {'cp','hp'}, use_global_device_ids=true, to_apply=%region_14.15 | all-reduce | flops 64 | bytes 512 | tf_op jit(solution)/shard_map/psum | solution.py:15
  437.9 7.5 fusion.69
  455.4 5.2 collective-permute-start.7
  460.6 71.0 %collective-permute-done.8 = bf16[14,1,128,512]{3,1,2,0:T(2,128)(2,1)S(1)} collective-permute-done((bf16[14,1,128,512]{3,1,2,0:T(2,128)(2,1)S(1)}, bf16[14,1,128,512]{3,1,2,0:T(2,128)(2,1)S(1)}, u32[]{:S(2)}, u32[]{:S(2)}) %collective-permute-start.8) | collective-permute-done | bytes 1835040 | tf_op jit(solution)/shard_map/ppermute | solution.py:52
  533.5 20.0 %maximum_bitcast_fusion.2 = bf16[14,3,1,128,512]{4,1,3,0,2:T(4,128)(2,1)} fusion(bf16[14,1,128,512]{3,1,2,0:T(2,128)(2,1)S(1)} %collective-permute-done.8, bf16[12,1,128,512]{3,1,2,0:T(2,128)(2,1)S(1)} %fusion.69, bf16[2,1,128,512]{3,1,2,0:T(2,128)(2,1)S(1)} %broadcast_select_fusion.1, bf16[14,1,128,512]{3,1,2,0:T(2,128)(2,1)S(1)} %collective-permute-done.7), kind=kLoop, calls=%fused_computation.19 | loop fusion | flops 22020096 | bytes 11010048 | tf_op jit(solution)/shard_map/broadcast_in_dim | solution.py:26
  553.5 10.0 %pad.4 = bf16[14,3,1,136,512]{4,1,3,0,2:T(4,128)(2,1)} pad(bf16[14,3,1,128,512]{4,1,3,0,2:T(4,128)(2,1)} %maximum_bitcast_fusion.2, bf16[]{:T(256)} %constant.27), padding=0_0x0_0x0_0x1_7x0_0 | pad | bytes 11354114 | tf_op jit(solution)/shard_map/broadcast_in_dim | solution.py:26
  571.0 32.2 %fusion.43 = (f32[512]{0:T(512)S(1)}, f32[512]{0:T(512)S(1)}, f32[12,1,8,17,512]{4,2,3,1,0:T(8,128)}) fusion(pred[8,17]{0,1:T(8,128)(4,1)S(1)} %copy-done.6, f32[512]{0:T(512)S(1)} %bitcast.229, bf16[4,3,3,3,512,512]{5,4,3,2,1,0:T(8,128)(2,1)} %param.6, bf16[14,3,1,7,2,512]{5,3,4,1,0,2:T(8,128)(2,1)S(1)} %slice.146, ...), kind=kOutput, calls=%fused_computation.52 | convolution fusion | flops 23129358336 | bytes 23955592 | tf_op jit(solution)/shard_map/conv_general_dilated | solution.py:26
  603.6 31.2 %psum.31 = f32[2,32]{1,0:T(2,128)S(1)} all-reduce(f32[2,32]{1,0:T(2,128)S(1)} %pad_maximum_fusion.7), channel_id=1, replica_groups=mesh['dp'=1,'hp'=2,'cp'=4] {'cp','hp'}, use_global_device_ids=true, to_apply=%region_19.20 | all-reduce | flops 64 | bytes 512 | tf_op jit(solution)/shard_map/psum | solution.py:15
  635.1 5.4 copy.19
  640.6 7.5 fusion.68
  658.1 5.2 collective-permute-start.10
  663.3 71.0 %collective-permute-done.11 = bf16[14,1,128,512]{3,1,2,0:T(2,128)(2,1)S(1)} collective-permute-done((bf16[14,1,128,512]{3,1,2,0:T(2,128)(2,1)S(1)}, bf16[14,1,128,512]{3,1,2,0:T(2,128)(2,1)S(1)}, u32[]{:S(2)}, u32[]{:S(2)}) %collective-permute-start.11) | collective-permute-done | bytes 1835040 | tf_op jit(solution)/shard_map/ppermute | solution.py:52
  736.3 20.0 %maximum_bitcast_fusion.3 = bf16[14,3,1,128,512]{4,1,3,0,2:T(4,128)(2,1)} fusion(bf16[14,1,128,512]{3,1,2,0:T(2,128)(2,1)S(1)} %collective-permute-done.11, bf16[12,1,128,512]{3,1,2,0:T(2,128)(2,1)S(1)} %fusion.68, bf16[2,1,128,512]{3,1,2,0:T(2,128)(2,1)S(1)} %broadcast_select_fusion, bf16[14,1,128,512]{3,1,2,0:T(2,128)(2,1)S(1)} %collective-permute-done.10), kind=kLoop, calls=%fused_computation.20 | loop fusion | flops 22020096 | bytes 11010048 | tf_op jit(solution)/shard_map/broadcast_in_dim | solution.py:26
  756.2 10.0 %pad.6 = bf16[14,3,1,136,512]{4,1,3,0,2:T(4,128)(2,1)} pad(bf16[14,3,1,128,512]{4,1,3,0,2:T(4,128)(2,1)} %maximum_bitcast_fusion.3, bf16[]{:T(256)} %constant.27), padding=0_0x0_0x0_0x1_7x0_0 | pad | bytes 11354114 | tf_op jit(solution)/shard_map/broadcast_in_dim | solution.py:26
  771.2 26.8 %fusion.88 = f32[12,1,8,17,512]{4,2,3,1,0:T(8,128)S(1)} fusion(bf16[4,3,3,3,512,512]{5,4,3,2,1,0:T(8,128)(2,1)} %param.6, bf16[14,3,1,7,2,512]{5,3,4,1,0,2:T(8,128)(2,1)S(1)} %slice.150, bf16[14,3,1,8,17,512]{5,3,4,1,0,2:T(8,128)(2,1)S(1)} %copy.23, pred[8,17]{0,1:T(8,128)(4,1)S(1)} %copy-done.6), kind=kOutput, calls=%fused_computation.99 | convolution fusion | flops 23122673664 | bytes 23949448 | tf_op jit(solution)/shard_map/conv_general_dilated | solution.py:26
  (109 shorter events, 90.2 us)
Async XLA Ops:
  44.9 2.8 collective-permute-start
  48.4 11.3 %copy-start.3 = (f32[4,512]{1,0:T(4,128)S(1)}, f32[4,512]{1,0:T(4,128)}, u32[]{:S(2)}) copy-start(f32[4,512]{1,0:T(4,128)} %param.7) | copy-start | bytes 24580
  53.1 76.5 %collective-permute-start.2 = (bf16[14,1,128,512]{3,1,2,0:T(2,128)(2,1)S(1)}, bf16[14,1,128,512]{3,1,2,0:T(2,128)(2,1)S(1)}, u32[]{:S(2)}, u32[]{:S(2)}) collective-permute-start(bf16[14,1,128,512]{3,1,2,0:T(2,128)(2,1)S(1)} %pad_maximum_fusion), channel_id=1, source_target_pairs={{4,0},{5,1},{6,2},{7,3}} | collective-permute-start | bytes 5505032 | tf_op jit(solution)/shard_map/ppermute | solution.py:52
  54.4 77.1 %collective-permute-start.1 = (bf16[14,1,128,512]{3,1,2,0:T(2,128)(2,1)S(1)}, bf16[14,1,128,512]{3,1,2,0:T(2,128)(2,1)S(1)}, u32[]{:S(2)}, u32[]{:S(2)}) collective-permute-start(bf16[14,1,128,512]{3,1,2,0:T(2,128)(2,1)S(1)} %pad_maximum_fusion), channel_id=1, source_target_pairs={{0,4},{1,5},{2,6},{3,7}} | collective-permute-start | bytes 5505032 | tf_op jit(solution)/shard_map/ppermute | solution.py:51
  161.5 5.0 copy-start.6
  244.6 2.8 collective-permute-start.3
  252.8 77.5 %collective-permute-start.5 = (bf16[14,1,128,512]{3,1,2,0:T(2,128)(2,1)S(1)}, bf16[14,1,128,512]{3,1,2,0:T(2,128)(2,1)S(1)}, u32[]{:S(2)}, u32[]{:S(2)}) collective-permute-start(bf16[14,1,128,512]{3,1,2,0:T(2,128)(2,1)S(1)} %pad_maximum_fusion.1), channel_id=1, source_target_pairs={{4,0},{5,1},{6,2},{7,3}} | collective-permute-start | bytes 5505032 | tf_op jit(solution)/shard_map/ppermute | solution.py:52
  254.1 78.2 %collective-permute-start.4 = (bf16[14,1,128,512]{3,1,2,0:T(2,128)(2,1)S(1)}, bf16[14,1,128,512]{3,1,2,0:T(2,128)(2,1)S(1)}, u32[]{:S(2)}, u32[]{:S(2)}) collective-permute-start(bf16[14,1,128,512]{3,1,2,0:T(2,128)(2,1)S(1)} %pad_maximum_fusion.1), channel_id=1, source_target_pairs={{0,4},{1,5},{2,6},{3,7}} | collective-permute-start | bytes 5505032 | tf_op jit(solution)/shard_map/ppermute | solution.py:51
  395.5 3.5 copy-start
  445.9 2.8 collective-permute-start.6
  454.1 77.5 %collective-permute-start.8 = (bf16[14,1,128,512]{3,1,2,0:T(2,128)(2,1)S(1)}, bf16[14,1,128,512]{3,1,2,0:T(2,128)(2,1)S(1)}, u32[]{:S(2)}, u32[]{:S(2)}) collective-permute-start(bf16[14,1,128,512]{3,1,2,0:T(2,128)(2,1)S(1)} %pad_maximum_fusion.2), channel_id=1, source_target_pairs={{4,0},{5,1},{6,2},{7,3}} | collective-permute-start | bytes 5505032 | tf_op jit(solution)/shard_map/ppermute | solution.py:52
  455.4 78.2 %collective-permute-start.7 = (bf16[14,1,128,512]{3,1,2,0:T(2,128)(2,1)S(1)}, bf16[14,1,128,512]{3,1,2,0:T(2,128)(2,1)S(1)}, u32[]{:S(2)}, u32[]{:S(2)}) collective-permute-start(bf16[14,1,128,512]{3,1,2,0:T(2,128)(2,1)S(1)} %pad_maximum_fusion.2), channel_id=1, source_target_pairs={{0,4},{1,5},{2,6},{3,7}} | collective-permute-start | bytes 5505032 | tf_op jit(solution)/shard_map/ppermute | solution.py:51
  568.3 2.5 copy-start.1
  603.2 37.4 %copy-start.4 = (f32[1,512]{1,0:T(1,128)S(1)}, f32[1,512]{1,0:T(1,128)}, u32[]{:S(2)}) copy-start(f32[1,512]{1,0:T(1,128)} %get-tuple-element.26) | copy-start | bytes 6148
  603.2 37.4 %copy-start.5 = (f32[1,512]{1,0:T(1,128)S(1)}, f32[1,512]{1,0:T(1,128)}, u32[]{:S(2)}) copy-start(f32[1,512]{1,0:T(1,128)} %get-tuple-element.30) | copy-start | bytes 6148
  648.6 2.8 collective-permute-start.9
  656.8 77.5 %collective-permute-start.11 = (bf16[14,1,128,512]{3,1,2,0:T(2,128)(2,1)S(1)}, bf16[14,1,128,512]{3,1,2,0:T(2,128)(2,1)S(1)}, u32[]{:S(2)}, u32[]{:S(2)}) collective-permute-start(bf16[14,1,128,512]{3,1,2,0:T(2,128)(2,1)S(1)} %pad_maximum_fusion.3), channel_id=1, source_target_pairs={{4,0},{5,1},{6,2},{7,3}} | collective-permute-start | bytes 5505032 | tf_op jit(solution)/shard_map/ppermute | solution.py:52
  658.1 78.2 %collective-permute-start.10 = (bf16[14,1,128,512]{3,1,2,0:T(2,128)(2,1)S(1)}, bf16[14,1,128,512]{3,1,2,0:T(2,128)(2,1)S(1)}, u32[]{:S(2)}, u32[]{:S(2)}) collective-permute-start(bf16[14,1,128,512]{3,1,2,0:T(2,128)(2,1)S(1)} %pad_maximum_fusion.3), channel_id=1, source_target_pairs={{0,4},{1,5},{2,6},{3,7}} | collective-permute-start | bytes 5505032 | tf_op jit(solution)/shard_map/ppermute | solution.py:51
  798.0 3.5 copy-start.2
where the time goes:
time: 821 us; the launch traced here: 808 us
  waiting for transfers between devices  294 us (36%)
  other arithmetic  151 us (18%)
  blocking collectives  121 us (15%)
  matrix products  118 us (14%)
  local copies, waits for them, and re-layouts  91.1 us (11%)
  starting transfers between devices  32.5 us (4%)
    ppermute x4, waiting for transfers between devices, local_decode(): from_below = lax.ppermute(extended[:, :1], 'hp', rows_up)  282 us
    psum x4, blocking collectives, norm_silu(): stat_sums = lax.psum(stat_sums, ('cp', 'hp'))  121 us
    conv_general_dilated x4, matrix products, conv_valid(): lax.conv_general_dilated(padded[None], kernel, (1, 1, 1), ((0, 0), (0, 0)...  118 us
    broadcast_in_dim x4, other arithmetic, conv_valid(): padded[None]  80 us
    broadcast_in_dim x4, local copies, waits for them, and re-layouts, conv_valid(): padded[None]  39.9 us
    conv_general_dilated x12, local copies, waits for them, and re-layouts, conv_valid(): lax.conv_general_dilated(padded[None], kernel, (1, 1, 1), ((0, 0), (0, 0)...  37.6 us
    convert_element_type x4, other arithmetic, norm_silu(): jax.nn.silu(local_act.astype(jnp.float32) * scale_c + shift_c)  30.9 us
    ppermute x4, starting transfers between devices, local_decode(): from_above = lax.ppermute(extended[:, row_count - 1:], 'hp', rows_down)  20.9 us
  transfers between devices with their start and end apart: 12, of which 12 were waited for; matrix products, arithmetic and copies ran while one was open for 0% of the time, Pallas kernels for 0%

commit v1 on v0

v1 whole, which is shorter than its diff:
```python
import functools

import jax
import jax.numpy as jnp
from jax import lax
from jax.experimental import pallas as pl
from jax.experimental.pallas import tpu as pltpu
from jax.sharding import PartitionSpec as P

GROUPS = 32
EPS = 1e-6
MESH = pl.DeviceIdType.MESH
F32 = jnp.float32
BF16 = jnp.bfloat16


def kernel(dims, lat, w_hbm, bias, gamma, beta, out, vid, act, acc, w_buf, x_in, halo, edge, ecol, s_acc, s_tot, s_send, s_recv,
           l_sem, w_sem, xs_sem, xr_sem, hs_sem, hr_sem, es_sem, er_sem, ei_sem, ss_sem, sr_sem, o_sem):
    n_cp, frames, half, chans, count = dims
    n_dev = 2 * n_cp
    n_pad = frames + 2
    h = lax.axis_index("hp")
    r = lax.axis_index("cp")
    other = 1 - h
    me = h * n_cp + r
    partner = {"hp": other, "cp": r}
    nxt = {"hp": h, "cp": lax.rem(r + 1, n_cp)}
    diag = {"hp": other, "cp": lax.rem(r + 1, n_cp)}
    not_last = r < n_cp - 1
    not_first = r > 0
    tail = pl.ds(frames - 2, 2)
    my_cols = pl.ds(pl.multiple_of(h * half, half), half)
    ot_cols = pl.ds(pl.multiple_of(other * half, half), half)

    def remote(src, dst, send, recv, dev):
        return pltpu.make_async_remote_copy(src_ref=src, dst_ref=dst, send_sem=send, recv_sem=recv, device_id=dev, device_id_type=MESH)

    def peer(step):
        t = lax.rem(me + step, n_dev)
        return {"hp": t // n_cp, "cp": lax.rem(t, n_cp)}

    load_x = pltpu.make_async_copy(lat, x_in, l_sem.at[0])
    load_own = pltpu.make_async_copy(lat.at[:, 0, my_cols, :], vid.at[0, h], l_sem.at[1])
    load_x.start()
    load_own.start()

    def w_copy(layer):
        slot = lax.rem(layer, 2)
        return pltpu.make_async_copy(w_hbm.at[layer], w_buf.at[slot], w_sem.at[slot])

    w_copy(0).start()
    w_copy(1).start()

    barrier = pltpu.get_barrier_semaphore()
    for step in range(1, n_dev):
        pl.semaphore_signal(barrier, inc=1, device_id=peer(step), device_id_type=MESH)
    pl.semaphore_wait(barrier, n_dev - 1)

    x_tail = remote(lat.at[tail, 0, ot_cols, :], vid.at[0, h, tail], xs_sem.at[0], xr_sem.at[0], partner)
    x_head = remote(lat.at[pl.ds(0, frames - 2), 0, ot_cols, :], vid.at[0, h, pl.ds(0, frames - 2)], xs_sem.at[1], xr_sem.at[1], partner)
    x_tail.start()
    x_head.start()
    x_halo = remote(lat.at[tail, 0, my_cols, :], halo.at[0, h], hs_sem.at[0], hr_sem.at[0, 0], nxt)

    @pl.when(not_last)
    def _():
        x_halo.start()

    s_acc[...] = jnp.zeros_like(s_acc)
    s_tot[...] = jnp.zeros_like(s_tot)
    load_x.wait()

    def fold(v):
        t = v[0:8]
        for k in range(1, v.shape[0] // 8):
            t = t + v[8 * k:8 * k + 8]
        return t

    def first_sums(f, carry):
        v = x_in[f, 0].astype(F32)
        s_acc[0] += fold(v)
        s_acc[1] += fold(v * v)
        lo, hi = v[half - 1:half], v[half:half + 1]
        ecol[h, f] = jnp.where(h == 0, lo, hi)
        edge[0, h, f + 2] = jnp.where(h == 0, hi, lo)
        return carry

    lax.fori_loop(0, frames, first_sums, 0)
    e_part = remote(ecol.at[h], edge.at[0, h, pl.ds(2, frames)], es_sem.at[0], ei_sem.at[0], partner)
    e_part.start()
    e_nxt = remote(edge.at[0, h, pl.ds(frames, 2)], edge.at[0, h, pl.ds(0, 2)], es_sem.at[1], ei_sem.at[1], nxt)
    e_diag = remote(ecol.at[h, tail], edge.at[0, h, pl.ds(0, 2)], es_sem.at[2], ei_sem.at[2], diag)

    @pl.when(not_last)
    def _():
        e_nxt.start()
        e_diag.start()

    def halo_send(slot, row, k):
        return remote(vid.at[slot, row, tail], halo.at[slot, row], hs_sem.at[k], hr_sem.at[slot, k], nxt)

    def edge_sends(slot):
        a = remote(ecol, edge.at[slot, :, pl.ds(2, frames)], es_sem.at[0], er_sem.at[slot, 0], partner)
        b = remote(ecol.at[:, tail], edge.at[slot, :, pl.ds(0, 2)], es_sem.at[1], er_sem.at[slot, 1], diag)
        return a, b

    def out_send():
        return remote(vid.at[0, other], out.at[:, 0, my_cols, :], o_sem.at[0], o_sem.at[1], partner)

    def out_local():
        return pltpu.make_async_copy(vid.at[0, h], out.at[:, 0, my_cols, :], o_sem.at[2])

    lane = lax.broadcasted_iota(jnp.int32, (8, chans), 1)
    rowid = lax.broadcasted_iota(jnp.int32, (half, chans), 0)
    n_group = chans // GROUPS

    def layer_body(layer, carry):
        slot = lax.rem(layer, 2)
        nslot = 1 - slot

        s_send[0:1] = jnp.sum(s_acc[0], axis=0, keepdims=True)
        s_send[1:2] = jnp.sum(s_acc[1], axis=0, keepdims=True)
        s_acc[...] = jnp.zeros_like(s_acc)
        sends = [remote(s_send, s_recv.at[slot, step], ss_sem.at[step], sr_sem.at[slot, step], peer(step)) for step in range(1, n_dev)]
        for c in sends:
            c.start()

        @pl.when(jnp.logical_and(layer >= 1, layer < 3))
        def _():
            w_copy(layer + 1).start()

        total = s_send[...]
        for c in sends:
            c.wait()
        for step in range(1, n_dev):
            total = total + s_recv[slot, step]
        s_tot[0:2] = total
        t = s_tot[...]
        shift_by = 1
        while shift_by < n_group:
            up = pltpu.roll(t, chans - shift_by, 1)
            down = pltpu.roll(t, shift_by, 1)
            t = t + jnp.where((lane & shift_by) == 0, up, down)
            shift_by *= 2
        t = t * (1.0 / count)
        mean = t[0:1]
        inv = lax.rsqrt(t[1:2] - mean * mean + EPS)
        scale = inv * gamma[layer]
        half_scale = 0.5 * scale
        half_shift = 0.5 * (beta[layer] - mean * scale)

        def silu(v):
            u = v * half_scale + half_shift
            return u + u * jnp.tanh(u)

        def norm_frame(v, e, row, f):
            y = silu(v.astype(F32))
            ye = silu(e)
            left = jnp.where(h == 0, 0.0, ye)
            right = jnp.where(h == 0, ye, 0.0)
            rows = pl.ds(pl.multiple_of(f * half, half), half)
            act[row, rows, 0:chans] = jnp.where(rowid == 0, left, pltpu.roll(y, 1, 0)).astype(BF16)
            act[row, rows, chans:2 * chans] = y.astype(BF16)
            act[row, rows, 2 * chans:3 * chans] = jnp.where(rowid == half - 1, right, pltpu.roll(y, half - 1, 0)).astype(BF16)

        def norm_row(row):
            @pl.when(r == 0)
            def _():
                for f in range(2):
                    halo[slot, row, f] = vid[slot, row, 0]
                    edge[slot, row, f] = edge[slot, row, 2]

            def past(f, c):
                norm_frame(halo[slot, row, f], edge[slot, row, f], row, f)
                return c

            def own(f, c):
                norm_frame(vid[slot, row, f], edge[slot, row, f + 2], row, f + 2)
                return c

            lax.fori_loop(0, 2, past, 0)
            lax.fori_loop(0, frames, own, 0)

        @pl.when(layer == 0)
        def _():
            load_own.wait()
            e_part.wait()

            @pl.when(not_last)
            def _():
                x_halo.wait_send()
                e_nxt.wait_send()
                e_diag.wait_send()

            @pl.when(not_first)
            def _():
                x_halo.wait_recv()
                e_nxt.wait_recv()
                e_diag.wait_recv()

            x_tail.wait()

            @pl.when(not_last)
            def _():
                halo_send(0, other, 1).start()

        @pl.when(layer > 0)
        def _():
            a, b = edge_sends(slot)
            a.wait()

            @pl.when(not_last)
            def _():
                b.wait_send()
                halo_send(slot, other, 0).wait_send()
                halo_send(slot, h, 1).wait_send()

            @pl.when(not_first)
            def _():
                b.wait_recv()
                halo_send(slot, other, 0).wait_recv()
                halo_send(slot, h, 1).wait_recv()

        def step_body(s, c):
            is0 = layer == 0
            hi = s // 2
            lo = lax.rem(s, 2)
            a_idx = jnp.where(is0, lo, hi)
            j_idx = jnp.where(is0, hi, lo)
            i_row = jnp.where(a_idx == 0, other, h)
            j_row = jnp.where(j_idx == 0, h, other)
            di = j_row - i_row + 1

            @pl.when(jnp.logical_and(is0, s == 2))
            def _():
                x_head.wait()

                @pl.when(not_last)
                def _():
                    halo_send(0, other, 1).wait_send()

                @pl.when(not_first)
                def _():
                    halo_send(0, other, 1).wait_recv()

            @pl.when(jnp.logical_or(s == 0, s == jnp.where(is0, 2, 1)))
            def _():
                norm_row(j_row)

            @pl.when(s == 0)
            def _():
                w_copy(layer).wait()

            d = jnp.where(j_idx == 0, 0.0, acc[i_row])
            p = None
            for k in range(3):
                q = jnp.dot(act[j_row, k * half:(k + frames) * half, :], w_buf[slot, k, di], preferred_element_type=F32)
                p = q if p is None else p + q
            acc[i_row] = d + p

            @pl.when(j_idx == 1)
            def _():
                def finish(f, c2):
                    rows = pl.ds(pl.multiple_of(f * half, half), half)
                    v = (acc[i_row, rows, :] + bias[layer]).astype(BF16).astype(F32)
                    res = vid[0, i_row, f].astype(F32)
                    vb = jnp.where(slot == 1, res + v, v).astype(BF16)
                    vid[nslot, i_row, f] = vb
                    v = vb.astype(F32)
                    s_acc[0] += fold(v)
                    s_acc[1] += fold(v * v)
                    ecol[i_row, f] = jnp.where(h == 0, v[half - 1:half], v[0:1])
                    return c2

                lax.fori_loop(0, frames, finish, 0)

                @pl.when(jnp.logical_and(layer < 3, not_last))
                def _():
                    remote(vid.at[nslot, i_row, tail], halo.at[nslot, i_row], hs_sem.at[a_idx], hr_sem.at[nslot, a_idx], nxt).start()

                @pl.when(jnp.logical_and(layer < 3, a_idx == 1))
                def _():
                    a, b = edge_sends(nslot)
                    a.start()

                    @pl.when(not_last)
                    def _():
                        b.start()

                @pl.when(jnp.logical_and(layer == 3, a_idx == 0))
                def _():
                    out_send().start()

                @pl.when(jnp.logical_and(layer == 3, a_idx == 1))
                def _():
                    out_local().start()

            return c

        lax.fori_loop(0, 4, step_body, 0)
        return carry

    lax.fori_loop(0, 4, layer_body, 0)
    out_local().wait()
    out_send().wait()


def solution(mesh):
    n_cp = mesh.shape["cp"]

    def local_decode(lat, conv_w, conv_b, gn_gamma, gn_beta):
        frames, _, width, chans = lat.shape
        half = width // 2
        n_dev = 2 * n_cp
        count = frames * n_cp * 2 * width * (chans // GROUPS)
        dma = pltpu.SemaphoreType.DMA
        any_spec = pl.BlockSpec(memory_space=pl.ANY)
        vmem = pl.BlockSpec(memory_space=pltpu.VMEM)
        return pl.pallas_call(
            functools.partial(kernel, (n_cp, frames, half, chans, count)),
            out_shape=jax.ShapeDtypeStruct(lat.shape, BF16),
            in_specs=[any_spec, any_spec, vmem, vmem, vmem],
            out_specs=any_spec,
            scratch_shapes=[
                pltpu.VMEM((2, 2, frames, half, chans), BF16),
                pltpu.VMEM((2, (frames + 2) * half, 3 * chans), BF16),
                pltpu.VMEM((2, frames * half, chans), F32),
                pltpu.VMEM((2, 3, 3, 3 * chans, chans), BF16),
                pltpu.VMEM(lat.shape, BF16),
                pltpu.VMEM((2, 2, 2, half, chans), BF16),
                pltpu.VMEM((2, 2, frames + 2, 1, chans), F32),
                pltpu.VMEM((2, frames, 1, chans), F32),
                pltpu.VMEM((2, 8, chans), F32),
                pltpu.VMEM((8, chans), F32),
                pltpu.VMEM((2, chans), F32),
                pltpu.VMEM((2, n_dev, 2, chans), F32),
                dma((2,)),
                dma((2,)),
                dma((2,)),
                dma((2,)),
                dma((2,)),
                dma((2, 2)),
                dma((3,)),
                dma((2, 2)),
                dma((3,)),
                dma((n_dev,)),
                dma((2, n_dev)),
                dma((3,)),
            ],
            compiler_params=pltpu.CompilerParams(collective_id=0, has_side_effects=True, vmem_limit_bytes=60 * 1024 * 1024),
            name="decode",
        )(
            lat,
            conv_w.reshape(4, 3, 3, 3 * chans, chans),
            conv_b.reshape(4, 1, chans),
            gn_gamma.reshape(4, 1, chans),
            gn_beta.reshape(4, 1, chans),
        )

    spec = P(("dp", "cp"), "hp", None, None)
    return jax.shard_map(local_decode, mesh=mesh, in_specs=(spec, P(), P(), P(), P()), out_specs=spec, check_vma=False)
```

time: 821 us -> 128 us (0.16); the launches traced: 808 us -> 128 us
  waiting for transfers between devices: 294 us -> 0 us
  other arithmetic: 151 us -> 0 us
  Pallas kernels: 0 us -> 122 us
  blocking collectives: 121 us -> 0 us
  matrix products: 118 us -> 0 us
  local copies, waits for them, and re-layouts: 91.1 us -> 6.55 us
  starting transfers between devices: 32.5 us -> 0 us
    ppermute x12 -> x0, waiting for transfers between devices: 294 us -> none  [the longest x4 282 us: local_decode(): from_below = lax.ppermute(extended[:, :1], 'hp', rows_up)]
    pallas_call x0 -> x1, Pallas kernels: none -> 122 us  [local_decode(): pl.pallas_call(functools.partial(kernel, (n_cp, frames, half, chans, coun...]
    psum x4 -> x0, blocking collectives: 121 us -> none  [norm_silu(): stat_sums = lax.psum(stat_sums, ('cp', 'hp'))]
    conv_general_dilated x4 -> x0, matrix products: 118 us -> none  [conv_valid(): lax.conv_general_dilated(padded[None], kernel, (1, 1, 1), ((0, 0), (0, 0)...]
    broadcast_in_dim x4 -> x0, other arithmetic: 80 us -> none  [conv_valid(): padded[None]]
    broadcast_in_dim x4 -> x0, local copies, waits for them, and re-layouts: 39.9 us -> none  [conv_valid(): padded[None]]
    conv_general_dilated x12 -> x0, local copies, waits for them, and re-layouts: 37.6 us -> none  [conv_valid(): lax.conv_general_dilated(padded[None], kernel, (1, 1, 1), ((0, 0), (0, 0)...]
    convert_element_type x5 -> x0, other arithmetic: 35.2 us -> none  [the longest x4 30.9 us: norm_silu(): jax.nn.silu(local_act.astype(jnp.float32) * scale_c + shift_c)]
  transfers between devices with their start and end apart: 12 -> 0, of which waited for: 12 -> 0; matrix products, arithmetic and copies ran while one was open for 0% -> 0% of each run, Pallas kernels for 0% -> 0%
where the time goes in v1:
time: 128 us
  Pallas kernels  122 us (95%)
  local copies, waits for them, and re-layouts  6.55 us (5%)
    pallas_call x1, Pallas kernels, local_decode(): pl.pallas_call(functools.partial(kernel, (n_cp, frames, half, chans, coun...  122 us
    unnamed x1, local copies, waits for them, and re-layouts  2.65 us

profile of v1, /device:TPU:0, one launch (start us, length us, event | category | flops | bytes accessed | tf_op | source)
XLA Modules:
  0.0 128.1 jit_solution(8757850398164521593)
XLA Ops:
  0.0 1.3 %reshape.13.bias = f32[4,1,512]{2,1,0:T(1,128)} reshape(f32[4,512]{1,0:T(4,128)} %param.7) | data formatting | bytes 16384 | tf_op jit(solution)/shard_map/reshape | solution.py:355
  1.3 1.3 %reshape.14.gamma = f32[4,1,512]{2,1,0:T(1,128)} reshape(f32[4,512]{1,0:T(4,128)} %param.8) | data formatting | bytes 16384 | tf_op jit(solution)/shard_map/reshape | solution.py:356
  2.6 1.3 %reshape.15.beta = f32[4,1,512]{2,1,0:T(1,128)} reshape(f32[4,512]{1,0:T(4,128)} %param.9) | data formatting | bytes 16384 | tf_op jit(solution)/shard_map/reshape | solution.py:357
  3.9 121.5 %decode.1 = bf16[12,1,128,512]{3,2,1,0:T(8,128)(2,1)} custom-call(bf16[12,1,128,512]{3,2,1,0:T(8,128)(2,1)} %lat.1, bf16[4,3,3,1536,512]{4,3,2,1,0:T(8,128)(2,1)} %bitcast.1, f32[4,1,512]{2,1,0:T(1,128)} %reshape.13.bias, f32[4,1,512]{2,1,0:T(1,128)} %reshape.14.gamma, f32[4,1,512]{2,1,0:T(1,128)} %reshape.15.beta), custom_call_target="tpu_custom_call" | custom-call | tf_op jit(solution)/shard_map/decode/pallas_call | solution.py:319
  125.4 2.7 %copy.7 = bf16[12,1,128,512]{3,2,1,0:T(8,128)(2,1)} copy(bf16[12,1,128,512]{3,2,1,0:T(8,128)(2,1)} %decode.1) | data formatting | bytes 3145728

commit v2 on v0

v2 whole, which is shorter than its diff:
```python
import functools

import jax
import jax.numpy as jnp
from jax import lax
from jax.experimental import pallas as pl
from jax.experimental.pallas import tpu as pltpu
from jax.sharding import PartitionSpec as P

GROUPS = 32
EPS = 1e-6
MESH = pl.DeviceIdType.MESH
F32 = jnp.float32
BF16 = jnp.bfloat16
OWN, OTH = 0, 1


def kernel(dims, lat, w_hbm, bias, gamma, beta, out, vid, act, acc, w_buf, x_in, halo, edge, ecol, s_acc, s_tot, s_send, s_recv,
           l_sem, w_sem, xs_sem, xr_sem, hs_sem, hr_sem, es_sem, er_sem, ss_sem, sr_sem, o_sem, os_sem, or_sem):
    n_cp, frames, half, chans, count = dims
    n_dev = 2 * n_cp
    per = frames // 4
    h = lax.axis_index("hp")
    r = lax.axis_index("cp")
    me = h * n_cp + r
    partner = {"hp": 1 - h, "cp": r}
    nxt = {"hp": h, "cp": lax.rem(r + 1, n_cp)}
    diag = {"hp": 1 - h, "cp": lax.rem(r + 1, n_cp)}
    not_last = r < n_cp - 1
    not_first = r > 0
    tail = pl.ds(frames - 2, 2)
    my_cols = pl.ds(pl.multiple_of(h * half, half), half)
    ot_cols = pl.ds(pl.multiple_of((1 - h) * half, half), half)

    def remote(src, dst, send, recv, dev):
        return pltpu.make_async_remote_copy(src_ref=src, dst_ref=dst, send_sem=send, recv_sem=recv, device_id=dev, device_id_type=MESH)

    def peer(step):
        t = lax.rem(me + step, n_dev)
        return {"hp": t // n_cp, "cp": lax.rem(t, n_cp)}

    load_x = pltpu.make_async_copy(lat, x_in, l_sem.at[0])
    load_own = pltpu.make_async_copy(lat.at[:, 0, my_cols, :], vid.at[0, OWN], l_sem.at[1])
    load_x.start()
    load_own.start()

    def w_copy(layer):
        slot = lax.rem(layer, 2)
        return pltpu.make_async_copy(w_hbm.at[layer], w_buf.at[slot], w_sem.at[slot])

    w_copy(0).start()

    barrier = pltpu.get_barrier_semaphore()
    for step in range(1, n_dev):
        pl.semaphore_signal(barrier, inc=1, device_id=peer(step), device_id_type=MESH)

    def fold(v):
        t = v[0:8]
        for k in range(1, v.shape[0] // 8):
            t = t + v[8 * k:8 * k + 8]
        return t

    s_acc[...] = jnp.zeros_like(s_acc)
    s_tot[...] = jnp.zeros_like(s_tot)
    load_x.wait()

    def first_sums(f, carry):
        v = x_in[f, 0].astype(F32)
        s_acc[0] += fold(v)
        s_acc[1] += fold(v * v)
        lo, hi = v[half - 1:half], v[half:half + 1]
        ecol[OWN, f] = jnp.where(h == 0, lo, hi)
        edge[0, OWN, f + 2] = jnp.where(h == 0, hi, lo)
        return carry

    lax.fori_loop(0, frames, first_sums, 0)
    pl.semaphore_wait(barrier, n_dev - 1)

    lane = lax.broadcasted_iota(jnp.int32, (8, chans), 1)
    rowid = lax.broadcasted_iota(jnp.int32, (half, chans), 0)
    n_group = chans // GROUPS

    def sum_sends(slot):
        return [remote(s_send, s_recv.at[slot, step], ss_sem.at[step], sr_sem.at[slot, step], peer(step)) for step in range(1, n_dev)]

    def sums_start(slot):
        s_send[0:1] = jnp.sum(s_acc[0], axis=0, keepdims=True)
        s_send[1:2] = jnp.sum(s_acc[1], axis=0, keepdims=True)
        s_acc[...] = jnp.zeros_like(s_acc)
        for c in sum_sends(slot):
            c.start()

    def sums_finish(slot, layer):
        total = s_send[...]
        for c in sum_sends(slot):
            c.wait()
        for step in range(1, n_dev):
            total = total + s_recv[slot, step]
        s_tot[0:2] = total
        t = s_tot[...]
        shift_by = 1
        while shift_by < n_group:
            up = pltpu.roll(t, chans - shift_by, 1)
            down = pltpu.roll(t, shift_by, 1)
            t = t + jnp.where((lane & shift_by) == 0, up, down)
            shift_by *= 2
        t = t * (1.0 / count)
        mean = t[0:1]
        inv = lax.rsqrt(t[1:2] - mean * mean + EPS)
        scale = inv * gamma[pl.ds(layer, 1), :]
        return 0.5 * scale, 0.5 * (beta[pl.ds(layer, 1), :] - mean * scale)

    def norm(coef, slot, row, p):
        def silu(v):
            u = v * coef[0] + coef[1]
            return u + u * jnp.tanh(u)

        v = halo[slot, row, p] if p < 2 else vid[slot, row, p - 2]
        y = silu(v.astype(F32))
        ye = silu(edge[slot, row, p])
        left = jnp.where(h == 0, 0.0, ye)
        right = jnp.where(h == 0, ye, 0.0)
        rows = pl.ds(p * half, half)
        act[row, rows, 0:chans] = jnp.where(rowid == 0, left, pltpu.roll(y, 1, 0)).astype(BF16)
        act[row, rows, chans:2 * chans] = y.astype(BF16)
        act[row, rows, 2 * chans:3 * chans] = jnp.where(rowid == half - 1, right, pltpu.roll(y, half - 1, 0)).astype(BF16)

    def dots(slot, i, js, lo, rows):
        total = None
        for j in js:
            di = 1 if i == j else (2 - 2 * h if i == OWN else 2 * h)
            for k in range(3):
                q = jnp.dot(act[j, pl.ds(lo + k * half, rows), :], w_buf[slot, k, di], preferred_element_type=F32)
                total = q if total is None else total + q
        return total

    def finish(layer, nslot, i, f0, p):
        b = bias[pl.ds(layer, 1), :]
        t1 = t2 = None
        for f in range(p.shape[0] // half):
            v = (p[f * half:(f + 1) * half] + b).astype(BF16).astype(F32)
            if isinstance(layer, int):
                vb = v.astype(BF16)
            else:
                res = vid[0, i, f0 + f].astype(F32)
                vb = jnp.where(nslot == 0, res + v, v).astype(BF16)
            vid[nslot, i, f0 + f] = vb
            v = vb.astype(F32)
            t1 = fold(v) if t1 is None else t1 + fold(v)
            t2 = fold(v * v) if t2 is None else t2 + fold(v * v)
            ecol[i, f0 + f] = jnp.where(h == 0, v[half - 1:half], v[0:1])
        s_acc[0] += t1
        s_acc[1] += t2

    def halo_send(slot, row):
        return remote(vid.at[slot, row, tail], halo.at[slot, row], hs_sem.at[row], hr_sem.at[slot, row], nxt)

    def edge_send(slot, row):
        return remote(ecol.at[row], edge.at[slot, 1 - row, pl.ds(2, frames)], es_sem.at[row, 0], er_sem.at[slot, 1 - row, 0], partner)

    def edge_diag(slot, row):
        return remote(ecol.at[row, tail], edge.at[slot, 1 - row, pl.ds(0, 2)], es_sem.at[row, 1], er_sem.at[slot, 1 - row, 1], diag)

    def edge_recv(slot, row):
        return edge_send(slot, 1 - row)

    def edge_diag_recv(slot, row):
        return edge_diag(slot, 1 - row)

    def repeat_first(slot, row):
        @pl.when(r == 0)
        def _():
            for f in range(2):
                halo[slot, row, f] = vid[slot, row, 0]
                edge[slot, row, f] = edge[slot, row, 2]

    pieces = [(0, 1), (1, per), (1 + per, per), (1 + 2 * per, frames - 1 - 2 * per)]

    def x_piece(g):
        f0, n = pieces[g]
        return remote(lat.at[pl.ds(f0, n), 0, ot_cols, :], vid.at[0, OTH, pl.ds(f0, n)], xs_sem.at[g], xr_sem.at[g], partner)

    sums_start(0)
    edge_send(0, OWN).start()
    x_halo = remote(lat.at[tail, 0, my_cols, :], halo.at[0, OWN], hs_sem.at[OWN], hr_sem.at[0, OWN], nxt)
    e_nxt = remote(edge.at[0, OWN, pl.ds(frames, 2)], edge.at[0, OWN, pl.ds(0, 2)], es_sem.at[OTH, 1], er_sem.at[0, OWN, 1], nxt)

    @pl.when(not_last)
    def _():
        edge_diag(0, OWN).start()
        e_nxt.start()
        x_halo.start()

    for g in (3, 2, 1, 0):
        x_piece(g).start()
    w_copy(1).start()
    load_own.wait()
    coef = sums_finish(0, 0)
    for p in range(2, frames + 2):
        norm(coef, 0, OWN, p)

    @pl.when(not_last)
    def _():
        x_halo.wait_send()
        e_nxt.wait_send()

    @pl.when(not_first)
    def _():
        x_halo.wait_recv()
        e_nxt.wait_recv()

    repeat_first(0, OWN)
    for p in range(2):
        norm(coef, 0, OWN, p)
    w_copy(0).wait()
    for i in (OTH, OWN):
        @pl.loop(0, 2)
        def _(c):
            lo = pl.multiple_of(c * (frames // 2) * half, half)
            acc[i, pl.ds(lo, frames // 2 * half), :] = dots(0, i, (OWN,), lo, frames // 2 * half)

    edge_send(0, OWN).wait_send()
    edge_recv(0, OTH).wait_recv()

    @pl.when(not_last)
    def _():
        edge_diag(0, OWN).wait_send()

    @pl.when(not_first)
    def _():
        edge_diag_recv(0, OTH).wait_recv()

    for g in (3, 2, 1, 0):
        x_piece(g).wait()
        if g == 3:
            @pl.when(not_last)
            def _():
                halo_send(0, OTH).start()
        if g == 0:
            @pl.when(not_first)
            def _():
                halo_send(0, OTH).wait_recv()

            repeat_first(0, OTH)
        for p in range(g * per, frames + 2 if g == 3 else (g + 1) * per):
            norm(coef, 0, OTH, p)
        rows = pl.ds(g * per * half, per * half)
        for i in (OTH, OWN):
            finish(0, 1, i, g * per, acc[i, rows, :] + dots(0, i, (OTH,), g * per * half, per * half))
        if g == 1:
            @pl.when(not_last)
            def _():
                halo_send(0, OTH).wait_send()
                halo_send(1, OTH).start()

    edge_send(1, OTH).start()

    @pl.when(not_last)
    def _():
        edge_diag(1, OTH).start()

    out_pieces = [(3 * per, per), (2 * per, per), (0, 2 * per)]

    def out_send(k):
        f0, n = out_pieces[k]
        return remote(vid.at[0, OTH, pl.ds(f0, n)], out.at[pl.ds(f0, n), 0, my_cols, :], os_sem.at[k], or_sem.at[k], partner)

    def out_local():
        return pltpu.make_async_copy(vid.at[0, OWN], out.at[:, 0, my_cols, :], o_sem.at[0])

    def layer_body(layer, carry):
        slot = lax.rem(layer, 2)
        nslot = 1 - slot
        last = layer == 3

        sums_start(slot)
        edge_send(slot, OWN).start()

        @pl.when(not_last)
        def _():
            edge_diag(slot, OWN).start()
            halo_send(slot, OWN).start()

        @pl.when(layer < 3)
        def _():
            w_copy(layer + 1).start()

        coef = sums_finish(slot, layer)
        edge_send(slot, OTH).wait_send()
        edge_recv(slot, OWN).wait_recv()
        edge_recv(slot, OTH).wait_recv()

        @pl.when(not_last)
        def _():
            edge_diag(slot, OTH).wait_send()
            halo_send(slot, OTH).wait_send()

        w_copy(layer).wait()

        def chunk(i, g):
            return dots(slot, i, (OWN, OTH), g * per * half, per * half)

        def norms(lo, hi):
            for p in range(lo, hi):
                for row in (OWN, OTH):
                    norm(coef, slot, row, p)

        norms(3 * per, frames + 2)
        p = chunk(OTH, 3)
        norms(2 * per, 3 * per)
        finish(layer, nslot, OTH, 3 * per, p)

        @pl.when(last)
        def _():
            out_send(0).start()

        p = chunk(OTH, 2)
        norms(per, 2 * per)
        finish(layer, nslot, OTH, 2 * per, p)

        @pl.when(last)
        def _():
            out_send(1).start()

        edge_send(slot, OWN).wait_send()

        @pl.when(not_last)
        def _():
            edge_diag(slot, OWN).wait_send()
            halo_send(slot, OWN).wait_send()

        @pl.when(not_first)
        def _():
            for row in (OWN, OTH):
                edge_diag_recv(slot, row).wait_recv()
                halo_send(slot, row).wait_recv()

        repeat_first(slot, OWN)
        repeat_first(slot, OTH)

        p = chunk(OTH, 1)
        norms(0, per)
        finish(layer, nslot, OTH, per, p)
        p = chunk(OTH, 0)
        finish(layer, nslot, OTH, 0, p)

        @pl.when(last)
        def _():
            out_send(2).start()

        @pl.when(jnp.logical_not(last))
        def _():
            edge_send(nslot, OTH).start()

            @pl.when(not_last)
            def _():
                edge_diag(nslot, OTH).start()
                halo_send(nslot, OTH).start()

        for g in (3, 2, 1, 0):
            p = chunk(OWN, g)
            finish(layer, nslot, OWN, g * per, p)
        return carry

    lax.fori_loop(1, 4, layer_body, 0)
    out_local().start()
    out_local().wait()
    for k in range(3):
        out_send(k).wait()


def solution(mesh):
    n_cp = mesh.shape["cp"]

    def local_decode(lat, conv_w, conv_b, gn_gamma, gn_beta):
        frames, _, width, chans = lat.shape
        half = width // 2
        n_dev = 2 * n_cp
        count = frames * n_cp * 2 * width * (chans // GROUPS)
        dma = pltpu.SemaphoreType.DMA
        any_spec = pl.BlockSpec(memory_space=pl.ANY)
        vmem = pl.BlockSpec(memory_space=pltpu.VMEM)
        return pl.pallas_call(
            functools.partial(kernel, (n_cp, frames, half, chans, count)),
            out_shape=jax.ShapeDtypeStruct(lat.shape, BF16),
            in_specs=[any_spec, any_spec, vmem, vmem, vmem],
            out_specs=any_spec,
            scratch_shapes=[
                pltpu.VMEM((2, 2, frames, half, chans), BF16),
                pltpu.VMEM((2, (frames + 2) * half, 3 * chans), BF16),
                pltpu.VMEM((2, frames * half, chans), F32),
                pltpu.VMEM((2, 3, 3, 3 * chans, chans), BF16),
                pltpu.VMEM(lat.shape, BF16),
                pltpu.VMEM((2, 2, 2, half, chans), BF16),
                pltpu.VMEM((2, 2, frames + 2, 1, chans), F32),
                pltpu.VMEM((2, frames, 1, chans), F32),
                pltpu.VMEM((2, 8, chans), F32),
                pltpu.VMEM((8, chans), F32),
                pltpu.VMEM((2, chans), F32),
                pltpu.VMEM((2, n_dev, 2, chans), F32),
                dma((2,)),
                dma((2,)),
                dma((4,)),
                dma((4,)),
                dma((2,)),
                dma((2, 2)),
                dma((2, 2)),
                dma((2, 2, 2)),
                dma((n_dev,)),
                dma((2, n_dev)),
                dma((1,)),
                dma((3,)),
                dma((3,)),
            ],
            compiler_params=pltpu.CompilerParams(collective_id=0, has_side_effects=True, vmem_limit_bytes=60 * 1024 * 1024),
            name="decode",
        )(lat, conv_w.reshape(4, 3, 3, 3 * chans, chans), conv_b, gn_gamma, gn_beta)

    spec = P(("dp", "cp"), "hp", None, None)
    return jax.shard_map(local_decode, mesh=mesh, in_specs=(spec, P(), P(), P(), P()), out_specs=spec, check_vma=False)
```

time: 821 us -> 97.2 us (0.12); the launches traced: 808 us -> 97 us
  waiting for transfers between devices: 294 us -> 0 us
  other arithmetic: 151 us -> 0 us
  blocking collectives: 121 us -> 0 us
  matrix products: 118 us -> 0 us
  Pallas kernels: 0 us -> 94.3 us
  local copies, waits for them, and re-layouts: 91.1 us -> 2.65 us
  starting transfers between devices: 32.5 us -> 0 us
    ppermute x12 -> x0, waiting for transfers between devices: 294 us -> none  [the longest x4 282 us: local_decode(): from_below = lax.ppermute(extended[:, :1], 'hp', rows_up)]
    psum x4 -> x0, blocking collectives: 121 us -> none  [norm_silu(): stat_sums = lax.psum(stat_sums, ('cp', 'hp'))]
    conv_general_dilated x4 -> x0, matrix products: 118 us -> none  [conv_valid(): lax.conv_general_dilated(padded[None], kernel, (1, 1, 1), ((0, 0), (0, 0)...]
    pallas_call x0 -> x1, Pallas kernels: none -> 94.3 us  [local_decode(): pl.pallas_call(functools.partial(kernel, (n_cp, frames, half, chans, coun...]
    broadcast_in_dim x4 -> x0, other arithmetic: 80 us -> none  [conv_valid(): padded[None]]
    broadcast_in_dim x4 -> x0, local copies, waits for them, and re-layouts: 39.9 us -> none  [conv_valid(): padded[None]]
    conv_general_dilated x12 -> x0, local copies, waits for them, and re-layouts: 37.6 us -> none  [conv_valid(): lax.conv_general_dilated(padded[None], kernel, (1, 1, 1), ((0, 0), (0, 0)...]
    convert_element_type x5 -> x0, other arithmetic: 35.2 us -> none  [the longest x4 30.9 us: norm_silu(): jax.nn.silu(local_act.astype(jnp.float32) * scale_c + shift_c)]
  transfers between devices with their start and end apart: 12 -> 0, of which waited for: 12 -> 0; matrix products, arithmetic and copies ran while one was open for 0% -> 0% of each run, Pallas kernels for 0% -> 0%
where the time goes in v2:
time: 97.2 us; the launch traced here: 97 us
  Pallas kernels  94.3 us (97%)
  local copies, waits for them, and re-layouts  2.65 us (3%)
    pallas_call x1, Pallas kernels, local_decode(): pl.pallas_call(functools.partial(kernel, (n_cp, frames, half, chans, coun...  94.3 us
    unnamed x1, local copies, waits for them, and re-layouts  2.65 us

profile of v2, /device:TPU:0, one launch (start us, length us, event | category | flops | bytes accessed | tf_op | source)
XLA Modules:
  0.0 97.0 jit_solution(3467596865025589629)
XLA Ops:
  0.0 94.3 %decode.1 = bf16[12,1,128,512]{3,2,1,0:T(8,128)(2,1)} custom-call(bf16[12,1,128,512]{3,2,1,0:T(8,128)(2,1)} %lat.1, bf16[4,3,3,1536,512]{4,3,2,1,0:T(8,128)(2,1)} %bitcast.1, f32[4,512]{1,0:T(4,128)} %bias.1, f32[4,512]{1,0:T(4,128)} %gamma.1, f32[4,512]{1,0:T(4,128)} %beta.1), custom_call_target="tpu_custom_call" | custom-call | tf_op jit(solution)/shard_map/decode/pallas_call | solution.py:383
  94.3 2.7 %copy.7 = bf16[12,1,128,512]{3,2,1,0:T(8,128)(2,1)} copy(bf16[12,1,128,512]{3,2,1,0:T(8,128)(2,1)} %decode.1) | data formatting | bytes 3145728

commit v3 on v2

--- a/solution.py
+++ b/solution.py
@@ -15,9 +15,10 @@
 OWN, OTH = 0, 1
 
 
-def kernel(dims, lat, w_hbm, bias, gamma, beta, out, vid, act, acc, w_buf, x_in, halo, edge, ecol, s_acc, s_tot, s_send, s_recv,
-           l_sem, w_sem, xs_sem, xr_sem, hs_sem, hr_sem, es_sem, er_sem, ss_sem, sr_sem, o_sem, os_sem, or_sem):
-    n_cp, frames, half, chans, count = dims
+def kernel(dims, lat, w_hbm, bias, gamma, beta, out, vid, act, acc, w_buf, x_in, halo, edge, ecol, ext, xact, edge2, ecol2, xres,
+           s_acc, s_tot, s_send, s_recv, l_sem, w_sem, xs_sem, xr_sem, hs_sem, hr_sem, es_sem, er_sem, ts_sem, tr_sem, cs_sem, cr_sem,
+           rs_sem, ss_sem, sr_sem, o_sem, os_sem, or_sem):
+    n_cp, frames, half, strip, chans, count = dims
     n_dev = 2 * n_cp
     per = frames // 4
     h = lax.axis_index("hp")
@@ -31,6 +32,9 @@
     tail = pl.ds(frames - 2, 2)
     my_cols = pl.ds(pl.multiple_of(h * half, half), half)
     ot_cols = pl.ds(pl.multiple_of((1 - h) * half, half), half)
+    part = half - strip
+    part_cols = pl.ds(pl.multiple_of(h * strip, strip), part)
+    edge_strip = pl.ds(pl.multiple_of((1 - h) * part, strip), strip)
 
     def remote(src, dst, send, recv, dev):
         return pltpu.make_async_remote_copy(src_ref=src, dst_ref=dst, send_sem=send, recv_sem=recv, device_id=dev, device_id_type=MESH)
@@ -77,7 +81,6 @@
     pl.semaphore_wait(barrier, n_dev - 1)
 
     lane = lax.broadcasted_iota(jnp.int32, (8, chans), 1)
-    rowid = lax.broadcasted_iota(jnp.int32, (half, chans), 0)
     n_group = chans // GROUPS
 
     def sum_sends(slot):
@@ -110,29 +113,45 @@
         scale = inv * gamma[pl.ds(layer, 1), :]
         return 0.5 * scale, 0.5 * (beta[pl.ds(layer, 1), :] - mean * scale)
 
+    def silu(coef, v):
+        u = v * coef[0] + coef[1]
+        return u + u * jnp.tanh(u)
+
+    def put_shifted(dst, row, p, y, left, right):
+        n = y.shape[0]
+        at = lax.broadcasted_iota(jnp.int32, y.shape, 0)
+        dst[row, p, :, 0:chans] = jnp.where(at == 0, left, pltpu.roll(y, 1, 0)).astype(BF16)
+        dst[row, p, :, chans:2 * chans] = y.astype(BF16)
+        dst[row, p, :, 2 * chans:3 * chans] = jnp.where(at == n - 1, right, pltpu.roll(y, n - 1, 0)).astype(BF16)
+
     def norm(coef, slot, row, p):
-        def silu(v):
-            u = v * coef[0] + coef[1]
-            return u + u * jnp.tanh(u)
-
         v = halo[slot, row, p] if p < 2 else vid[slot, row, p - 2]
-        y = silu(v.astype(F32))
-        ye = silu(edge[slot, row, p])
-        left = jnp.where(h == 0, 0.0, ye)
-        right = jnp.where(h == 0, ye, 0.0)
-        rows = pl.ds(p * half, half)
-        act[row, rows, 0:chans] = jnp.where(rowid == 0, left, pltpu.roll(y, 1, 0)).astype(BF16)
-        act[row, rows, chans:2 * chans] = y.astype(BF16)
-        act[row, rows, 2 * chans:3 * chans] = jnp.where(rowid == half - 1, right, pltpu.roll(y, half - 1, 0)).astype(BF16)
-
-    def dots(slot, i, js, lo, rows):
+        y = silu(coef, v.astype(F32))
+        ye = silu(coef, edge[slot, row, p])
+        put_shifted(act, row, p, y, jnp.where(h == 0, 0.0, ye), jnp.where(h == 0, ye, 0.0))
+
+    def norm_ext(coef, row, p):
+        mine = silu(coef, (halo[1, row, p] if p < 2 else vid[1, row, p - 2]).astype(F32))
+        y = silu(coef, ext[row, p].astype(F32))
+        far = silu(coef, edge2[row, p])
+        put_shifted(xact, row, p, y, jnp.where(h == 0, mine[half - 1:half], far), jnp.where(h == 0, far, mine[0:1]))
+
+    def dots(slot, i, js, lhs):
         total = None
         for j in js:
-            di = 1 if i == j else (2 - 2 * h if i == OWN else 2 * h)
+            if isinstance(i, int):
+                di = 1 if i == j else (2 - 2 * h if i == OWN else 2 * h)
+            else:
+                di = jnp.where(i == OWN, 1, 2 * h)
             for k in range(3):
-                q = jnp.dot(act[j, pl.ds(lo + k * half, rows), :], w_buf[slot, k, di], preferred_element_type=F32)
+                v = lhs(j, k)
+                v = v.reshape(v.shape[0] * v.shape[1], v.shape[2])
+                q = jnp.dot(v, w_buf[slot, k, di], preferred_element_type=F32)
                 total = q if total is None else total + q
         return total
+
+    def frames_of(f0, n):
+        return lambda j, k: act[j, pl.ds(f0 + k, n)]
 
     def finish(layer, nslot, i, f0, p):
         b = bias[pl.ds(layer, 1), :]
@@ -213,11 +232,13 @@
     for p in range(2):
         norm(coef, 0, OWN, p)
     w_copy(0).wait()
-    for i in (OTH, OWN):
-        @pl.loop(0, 2)
-        def _(c):
-            lo = pl.multiple_of(c * (frames // 2) * half, half)
-            acc[i, pl.ds(lo, frames // 2 * half), :] = dots(0, i, (OWN,), lo, frames // 2 * half)
+
+    @pl.loop(0, 4)
+    def _(c):
+        i = c // 2
+        f0 = lax.rem(c, 2) * (frames // 2)
+        rows = pl.ds(pl.multiple_of(f0 * half, half), frames // 2 * half)
+        acc[i, rows, :] = dots(0, i, (OWN,), frames_of(f0, frames // 2))
 
     edge_send(0, OWN).wait_send()
     edge_recv(0, OTH).wait_recv()
@@ -246,7 +267,7 @@
             norm(coef, 0, OTH, p)
         rows = pl.ds(g * per * half, per * half)
         for i in (OTH, OWN):
-            finish(0, 1, i, g * per, acc[i, rows, :] + dots(0, i, (OTH,), g * per * half, per * half))
+            finish(0, 1, i, g * per, acc[i, rows, :] + dots(0, i, (OTH,), frames_of(g * per, per)))
         if g == 1:
             @pl.when(not_last)
             def _():
@@ -259,112 +280,204 @@
     def _():
         edge_diag(1, OTH).start()
 
-    out_pieces = [(3 * per, per), (2 * per, per), (0, 2 * per)]
-
-    def out_send(k):
-        f0, n = out_pieces[k]
-        return remote(vid.at[0, OTH, pl.ds(f0, n)], out.at[pl.ds(f0, n), 0, my_cols, :], os_sem.at[k], or_sem.at[k], partner)
-
-    def out_local():
-        return pltpu.make_async_copy(vid.at[0, OWN], out.at[:, 0, my_cols, :], o_sem.at[0])
+    def strip_send(row):
+        return remote(vid.at[1, row, :, edge_strip, :], ext.at[1 - row, pl.ds(2, frames)], ts_sem.at[row, 0], tr_sem.at[1 - row, 0], partner)
+
+    def strip_diag(row):
+        return remote(vid.at[1, row, tail, edge_strip, :], ext.at[1 - row, pl.ds(0, 2)], ts_sem.at[row, 1], tr_sem.at[1 - row, 1], diag)
+
+    def col2_send(row):
+        return remote(ecol2.at[row], edge2.at[1 - row, pl.ds(2, frames)], cs_sem.at[row, 0], cr_sem.at[1 - row, 0], partner)
+
+    def col2_diag(row):
+        return remote(ecol2.at[row, tail], edge2.at[1 - row, pl.ds(0, 2)], cs_sem.at[row, 1], cr_sem.at[1 - row, 1], diag)
+
+    def res_send():
+        return remote(vid.at[0, OTH, :, edge_strip, :], xres, rs_sem.at[0], rs_sem.at[1], partner)
+
+    def head(slot, layer):
+        sums_start(slot)
+        edge_send(slot, OWN).start()
+
+        @pl.when(not_last)
+        def _():
+            edge_diag(slot, OWN).start()
+            halo_send(slot, OWN).start()
+
+    def head_finish(slot, layer):
+        coef = sums_finish(slot, layer)
+        for row in (OTH, OWN):
+            edge_send(slot, row).wait_send()
+            edge_recv(slot, row).wait_recv()
+
+        @pl.when(not_last)
+        def _():
+            for row in (OTH, OWN):
+                edge_diag(slot, row).wait_send()
+                halo_send(slot, row).wait_send()
+
+        @pl.when(not_first)
+        def _():
+            for row in (OTH, OWN):
+                edge_diag_recv(slot, row).wait_recv()
+                halo_send(slot, row).wait_recv()
+
+        repeat_first(slot, OWN)
+        repeat_first(slot, OTH)
+        w_copy(layer).wait()
+        return coef
 
     def layer_body(layer, carry):
         slot = lax.rem(layer, 2)
         nslot = 1 - slot
-        last = layer == 3
-
-        sums_start(slot)
-        edge_send(slot, OWN).start()
+        head(slot, layer)
+
+        @pl.when(layer == 2)
+        def _():
+            res_send().start()
+
+        w_copy(layer + 1).start()
+        coef = head_finish(slot, layer)
+
+        def norms(lo, hi):
+            for row in (OWN, OTH):
+                for p in range(lo, hi):
+                    norm(coef, slot, row, p)
+
+        def chunk(i, g):
+            finish(layer, nslot, i, g * per, dots(slot, i, (OWN, OTH), frames_of(g * per, per)))
+
+        norms(3 * per, frames + 2)
+        norms(2 * per, 3 * per)
+        chunk(OTH, 3)
+        norms(per, 2 * per)
+        chunk(OTH, 2)
+        norms(0, per)
+        chunk(OTH, 1)
+        chunk(OTH, 0)
+        edge_send(nslot, OTH).start()
 
         @pl.when(not_last)
         def _():
-            edge_diag(slot, OWN).start()
-            halo_send(slot, OWN).start()
-
-        @pl.when(layer < 3)
-        def _():
-            w_copy(layer + 1).start()
-
-        coef = sums_finish(slot, layer)
-        edge_send(slot, OTH).wait_send()
-        edge_recv(slot, OWN).wait_recv()
-        edge_recv(slot, OTH).wait_recv()
-
-        @pl.when(not_last)
-        def _():
-            edge_diag(slot, OTH).wait_send()
-            halo_send(slot, OTH).wait_send()
-
-        w_copy(layer).wait()
-
-        def chunk(i, g):
-            return dots(slot, i, (OWN, OTH), g * per * half, per * half)
-
-        def norms(lo, hi):
-            for p in range(lo, hi):
-                for row in (OWN, OTH):
-                    norm(coef, slot, row, p)
-
-        norms(3 * per, frames + 2)
-        p = chunk(OTH, 3)
-        norms(2 * per, 3 * per)
-        finish(layer, nslot, OTH, 3 * per, p)
-
-        @pl.when(last)
-        def _():
-            out_send(0).start()
-
-        p = chunk(OTH, 2)
-        norms(per, 2 * per)
-        finish(layer, nslot, OTH, 2 * per, p)
-
-        @pl.when(last)
-        def _():
-            out_send(1).start()
-
-        edge_send(slot, OWN).wait_send()
-
-        @pl.when(not_last)
-        def _():
-            edge_diag(slot, OWN).wait_send()
-            halo_send(slot, OWN).wait_send()
-
-        @pl.when(not_first)
-        def _():
-            for row in (OWN, OTH):
-                edge_diag_recv(slot, row).wait_recv()
-                halo_send(slot, row).wait_recv()
-
-        repeat_first(slot, OWN)
-        repeat_first(slot, OTH)
-
-        p = chunk(OTH, 1)
-        norms(0, per)
-        finish(layer, nslot, OTH, per, p)
-        p = chunk(OTH, 0)
-        finish(layer, nslot, OTH, 0, p)
-
-        @pl.when(last)
-        def _():
-            out_send(2).start()
-
-        @pl.when(jnp.logical_not(last))
-        def _():
-            edge_send(nslot, OTH).start()
+            edge_diag(nslot, OTH).start()
+            halo_send(nslot, OTH).start()
+
+        @pl.when(layer == 2)
+        def _():
+            strip_send(OTH).start()
 
             @pl.when(not_last)
             def _():
-                edge_diag(nslot, OTH).start()
-                halo_send(nslot, OTH).start()
+                strip_diag(OTH).start()
 
         for g in (3, 2, 1, 0):
-            p = chunk(OWN, g)
-            finish(layer, nslot, OWN, g * per, p)
+            chunk(OWN, g)
         return carry
 
-    lax.fori_loop(1, 4, layer_body, 0)
+    lax.fori_loop(1, 3, layer_body, 0)
+
+    wide = frames // 3
+
+    def out_send(k):
+        fs = pl.ds(k * wide, wide)
+        dst = out.at[fs, 0, pl.ds(pl.multiple_of(h * (half + strip), strip), part), :]
+        return remote(vid.at[0, OTH, fs, part_cols, :], dst, os_sem.at[k], or_sem.at[k], partner)
+
+    def out_local():
+        return pltpu.make_async_copy(vid.at[0, OWN], out.at[:, 0, my_cols, :], o_sem.at[0])
+
+    def out_ext():
+        dst = out.at[:, 0, pl.ds(pl.multiple_of(half - h * strip, strip), strip), :]
+        return pltpu.make_async_copy(xres, dst, o_sem.at[1])
+
+    head(1, 3)
+    strip_send(OWN).start()
+
+    @pl.when(not_last)
+    def _():
+        strip_diag(OWN).start()
+
+    def columns2(f, carry):
+        for row in (OWN, OTH):
+            v = vid[1, row, f, strip:half - strip, :].astype(F32)
+            ecol2[row, f] = jnp.where(h == 0, v[half - 2 * strip - 1:half - 2 * strip], v[0:1])
+        return carry
+
+    lax.fori_loop(0, frames, columns2, 0)
+    for row in (OWN, OTH):
+        col2_send(row).start()
+
+    @pl.when(not_last)
+    def _():
+        for row in (OWN, OTH):
+            col2_diag(row).start()
+
+    coef = head_finish(1, 3)
+
+    def norms(lo, hi):
+        for row in (OWN, OTH):
+            for p in range(lo, hi):
+                norm(coef, 1, row, p)
+
+    def close(res, p):
+        return (res.astype(F32) + (p + bias[3:4, :]).astype(BF16).astype(F32)).astype(BF16)
+
+    def part_chunk(k):
+        f0 = k * wide
+        p = dots(1, OTH, (OWN, OTH), lambda j, t: act[j, pl.ds(f0 + t, wide), part_cols, :])
+        for f in range(wide):
+            vid[0, OTH, f0 + f, part_cols, :] = close(vid[0, OTH, f0 + f, part_cols, :], p[f * part:(f + 1) * part])
+
+    def own_chunk(g):
+        p = dots(1, OWN, (OWN, OTH), frames_of(g * per, per))
+        for f in range(per):
+            vid[0, OWN, g * per + f] = close(vid[0, OWN, g * per + f], p[f * half:(f + 1) * half])
+
+    norms(2 * wide, frames + 2)
+    norms(wide, 2 * wide)
+    part_chunk(2)
+    out_send(2).start()
+    norms(0, wide)
+    part_chunk(1)
+    out_send(1).start()
+    part_chunk(0)
+    out_send(0).start()
+    for row in (OWN, OTH):
+        strip_send(row).wait()
+        col2_send(row).wait()
+
+    @pl.when(not_last)
+    def _():
+        for row in (OWN, OTH):
+            strip_diag(row).wait_send()
+            col2_diag(row).wait_send()
+
+    @pl.when(not_first)
+    def _():
+        for row in (OWN, OTH):
+            strip_diag(row).wait_recv()
+            col2_diag(row).wait_recv()
+
+    @pl.when(r == 0)
+    def _():
+        for row in (OWN, OTH):
+            for f in range(2):
+                ext[row, f] = ext[row, 2]
+                edge2[row, f] = edge2[row, 2]
+
+    res_send().wait()
+    for row in (OWN, OTH):
+        for p in range(frames + 2):
+            norm_ext(coef, row, p)
+    for g in (3, 2, 1, 0):
+        own_chunk(g)
+    p = dots(1, OWN, (OWN, OTH), lambda j, t: xact[j, pl.ds(t, frames)])
     out_local().start()
+    for f in range(frames):
+        xres[f] = close(xres[f], p[f * strip:(f + 1) * strip])
+    out_ext().start()
     out_local().wait()
+    out_ext().wait()
     for k in range(3):
         out_send(k).wait()
 
@@ -375,25 +488,31 @@
     def local_decode(lat, conv_w, conv_b, gn_gamma, gn_beta):
         frames, _, width, chans = lat.shape
         half = width // 2
+        strip = half // 4
         n_dev = 2 * n_cp
         count = frames * n_cp * 2 * width * (chans // GROUPS)
         dma = pltpu.SemaphoreType.DMA
         any_spec = pl.BlockSpec(memory_space=pl.ANY)
         vmem = pl.BlockSpec(memory_space=pltpu.VMEM)
         return pl.pallas_call(
-            functools.partial(kernel, (n_cp, frames, half, chans, count)),
+            functools.partial(kernel, (n_cp, frames, half, strip, chans, count)),
             out_shape=jax.ShapeDtypeStruct(lat.shape, BF16),
             in_specs=[any_spec, any_spec, vmem, vmem, vmem],
             out_specs=any_spec,
             scratch_shapes=[
                 pltpu.VMEM((2, 2, frames, half, chans), BF16),
-                pltpu.VMEM((2, (frames + 2) * half, 3 * chans), BF16),
+                pltpu.VMEM((2, frames + 2, half, 3 * chans), BF16),
                 pltpu.VMEM((2, frames * half, chans), F32),
                 pltpu.VMEM((2, 3, 3, 3 * chans, chans), BF16),
                 pltpu.VMEM(lat.shape, BF16),
                 pltpu.VMEM((2, 2, 2, half, chans), BF16),
                 pltpu.VMEM((2, 2, frames + 2, 1, chans), F32),
                 pltpu.VMEM((2, frames, 1, chans), F32),
+                pltpu.VMEM((2, frames + 2, strip, chans), BF16),
+                pltpu.VMEM((2, frames + 2, strip, 3 * chans), BF16),
+                pltpu.VMEM((2, frames + 2, 1, chans), F32),
+                pltpu.VMEM((2, frames, 1, chans), F32),
+                pltpu.VMEM((frames, strip, chans), BF16),
                 pltpu.VMEM((2, 8, chans), F32),
                 pltpu.VMEM((8, chans), F32),
                 pltpu.VMEM((2, chans), F32),
@@ -406,9 +525,14 @@
                 dma((2, 2)),
                 dma((2, 2)),
                 dma((2, 2, 2)),
+                dma((2, 2)),
+                dma((2, 2)),
+                dma((2, 2)),
+                dma((2, 2)),
+                dma((2,)),
                 dma((n_dev,)),
                 dma((2, n_dev)),
-                dma((1,)),
+                dma((2,)),
                 dma((3,)),
                 dma((3,)),
             ],

time: 97.2 us -> 91.5 us (0.941)
  Pallas kernels: 94.3 us -> 88.7 us
    pallas_call x1, Pallas kernels: 94.3 us -> 88.7 us  [local_decode(): pl.pallas_call(functools.partial(kernel, (n_cp, frames, half, strip, chan...]
where the time goes in v3:
time: 91.5 us; the launch traced here: 91.3 us
  Pallas kernels  88.7 us (97%)
  local copies, waits for them, and re-layouts  2.65 us (3%)
    pallas_call x1, Pallas kernels, local_decode(): pl.pallas_call(functools.partial(kernel, (n_cp, frames, half, strip, chan...  88.7 us
    unnamed x1, local copies, waits for them, and re-layouts  2.65 us

profile of v3, /device:TPU:0, one launch (start us, length us, event | category | flops | bytes accessed | tf_op | source)
XLA Modules:
  0.0 91.3 jit_solution(6321924823170400143)
XLA Ops:
  0.0 88.7 %decode.1 = bf16[12,1,128,512]{3,2,1,0:T(8,128)(2,1)} custom-call(bf16[12,1,128,512]{3,2,1,0:T(8,128)(2,1)} %lat.1, bf16[4,3,3,1536,512]{4,3,2,1,0:T(8,128)(2,1)} %bitcast.1, f32[4,512]{1,0:T(4,128)} %bias.1, f32[4,512]{1,0:T(4,128)} %gamma.1, f32[4,512]{1,0:T(4,128)} %beta.1), custom_call_target="tpu_custom_call" | custom-call | tf_op jit(solution)/shard_map/decode/pallas_call | solution.py:497
  88.7 2.7 %copy.7 = bf16[12,1,128,512]{3,2,1,0:T(8,128)(2,1)} copy(bf16[12,1,128,512]{3,2,1,0:T(8,128)(2,1)} %decode.1) | data formatting | bytes 3145728

commit v4 on v3

--- a/solution.py
+++ b/solution.py
@@ -15,7 +15,7 @@
 OWN, OTH = 0, 1
 
 
-def kernel(dims, lat, w_hbm, bias, gamma, beta, out, vid, act, acc, w_buf, x_in, halo, edge, ecol, ext, xact, edge2, ecol2, xres,
+def kernel(dims, lat, w_hbm, bias_hbm, gamma_hbm, beta_hbm, out, bias, gamma, beta, vid, act, acc, w_buf, x_in, halo, edge, ecol, ext, xact, edge2, ecol2, xres,
            s_acc, s_tot, s_send, s_recv, l_sem, w_sem, xs_sem, xr_sem, hs_sem, hr_sem, es_sem, er_sem, ts_sem, tr_sem, cs_sem, cr_sem,
            rs_sem, ss_sem, sr_sem, o_sem, os_sem, or_sem):
     n_cp, frames, half, strip, chans, count = dims
@@ -43,20 +43,26 @@
         t = lax.rem(me + step, n_dev)
         return {"hp": t // n_cp, "cp": lax.rem(t, n_cp)}
 
-    load_x = pltpu.make_async_copy(lat, x_in, l_sem.at[0])
-    load_own = pltpu.make_async_copy(lat.at[:, 0, my_cols, :], vid.at[0, OWN], l_sem.at[1])
-    load_x.start()
-    load_own.start()
+    def load_x(k):
+        fs = pl.ds(k * per, per)
+        return pltpu.make_async_copy(lat.at[fs], x_in.at[fs], l_sem.at[k])
+
+    for k in range(4):
+        load_x(k).start()
+    small = [pltpu.make_async_copy(a, b, l_sem.at[4 + k]) for k, (a, b) in enumerate([(bias_hbm, bias), (gamma_hbm, gamma), (beta_hbm, beta)])]
+    load_own = pltpu.make_async_copy(lat.at[:, 0, my_cols, :], vid.at[0, OWN], l_sem.at[7])
 
     def w_copy(layer):
         slot = lax.rem(layer, 2)
         return pltpu.make_async_copy(w_hbm.at[layer], w_buf.at[slot], w_sem.at[slot])
 
-    w_copy(0).start()
-
     barrier = pltpu.get_barrier_semaphore()
     for step in range(1, n_dev):
         pl.semaphore_signal(barrier, inc=1, device_id=peer(step), device_id_type=MESH)
+    for c in small:
+        c.start()
+    load_own.start()
+    w_copy(0).start()
 
     def fold(v):
         t = v[0:8]
@@ -66,7 +72,6 @@
 
     s_acc[...] = jnp.zeros_like(s_acc)
     s_tot[...] = jnp.zeros_like(s_tot)
-    load_x.wait()
 
     def first_sums(f, carry):
         v = x_in[f, 0].astype(F32)
@@ -77,7 +82,9 @@
         edge[0, OWN, f + 2] = jnp.where(h == 0, hi, lo)
         return carry
 
-    lax.fori_loop(0, frames, first_sums, 0)
+    for k in range(4):
+        load_x(k).wait()
+        lax.fori_loop(k * per, (k + 1) * per, first_sums, 0)
     pl.semaphore_wait(barrier, n_dev - 1)
 
     lane = lax.broadcasted_iota(jnp.int32, (8, chans), 1)
@@ -101,12 +108,16 @@
             total = total + s_recv[slot, step]
         s_tot[0:2] = total
         t = s_tot[...]
-        shift_by = 1
-        while shift_by < n_group:
-            up = pltpu.roll(t, chans - shift_by, 1)
-            down = pltpu.roll(t, shift_by, 1)
-            t = t + jnp.where((lane & shift_by) == 0, up, down)
-            shift_by *= 2
+        unit = 1
+        while unit < n_group:
+            place = (lane // unit) & 3
+            g = t
+            for d in range(1, 4):
+                up = pltpu.roll(t, chans - d * unit, 1)
+                down = pltpu.roll(t, (4 - d) * unit, 1)
+                g = g + jnp.where(place + d < 4, up, down)
+            t = g
+            unit *= 4
         t = t * (1.0 / count)
         mean = t[0:1]
         inv = lax.rsqrt(t[1:2] - mean * mean + EPS)
@@ -119,10 +130,14 @@
 
     def put_shifted(dst, row, p, y, left, right):
         n = y.shape[0]
-        at = lax.broadcasted_iota(jnp.int32, y.shape, 0)
-        dst[row, p, :, 0:chans] = jnp.where(at == 0, left, pltpu.roll(y, 1, 0)).astype(BF16)
+        at = lax.broadcasted_iota(jnp.int32, (8, chans), 0)
+        before = pltpu.roll(y, 1, 0)
+        after = pltpu.roll(y, n - 1, 0)
+        before = jnp.concatenate([jnp.where(at == 0, left, before[0:8]), before[8:]], axis=0)
+        after = jnp.concatenate([after[:n - 8], jnp.where(at == 7, right, after[n - 8:])], axis=0)
+        dst[row, p, :, 0:chans] = before.astype(BF16)
         dst[row, p, :, chans:2 * chans] = y.astype(BF16)
-        dst[row, p, :, 2 * chans:3 * chans] = jnp.where(at == n - 1, right, pltpu.roll(y, n - 1, 0)).astype(BF16)
+        dst[row, p, :, 2 * chans:3 * chans] = after.astype(BF16)
 
     def norm(coef, slot, row, p):
         v = halo[slot, row, p] if p < 2 else vid[slot, row, p - 2]
@@ -143,7 +158,7 @@
                 di = 1 if i == j else (2 - 2 * h if i == OWN else 2 * h)
             else:
                 di = jnp.where(i == OWN, 1, 2 * h)
-            for k in range(3):
+            for k in (2, 1, 0):
                 v = lhs(j, k)
                 v = v.reshape(v.shape[0] * v.shape[1], v.shape[2])
                 q = jnp.dot(v, w_buf[slot, k, di], preferred_element_type=F32)
@@ -214,6 +229,8 @@
         x_piece(g).start()
     w_copy(1).start()
     load_own.wait()
+    for c in small:
+        c.wait()
     coef = sums_finish(0, 0)
     for p in range(2, frames + 2):
         norm(coef, 0, OWN, p)
@@ -341,7 +358,7 @@
 
         def norms(lo, hi):
             for row in (OWN, OTH):
-                for p in range(lo, hi):
+                for p in reversed(range(lo, hi)):
                     norm(coef, slot, row, p)
 
         def chunk(i, g):
@@ -416,7 +433,7 @@
 
     def norms(lo, hi):
         for row in (OWN, OTH):
-            for p in range(lo, hi):
+            for p in reversed(range(lo, hi)):
                 norm(coef, 1, row, p)
 
     def close(res, p):
@@ -493,13 +510,15 @@
         count = frames * n_cp * 2 * width * (chans // GROUPS)
         dma = pltpu.SemaphoreType.DMA
         any_spec = pl.BlockSpec(memory_space=pl.ANY)
-        vmem = pl.BlockSpec(memory_space=pltpu.VMEM)
         return pl.pallas_call(
             functools.partial(kernel, (n_cp, frames, half, strip, chans, count)),
             out_shape=jax.ShapeDtypeStruct(lat.shape, BF16),
-            in_specs=[any_spec, any_spec, vmem, vmem, vmem],
+            in_specs=[any_spec] * 5,
             out_specs=any_spec,
             scratch_shapes=[
+                pltpu.VMEM(conv_b.shape, F32),
+                pltpu.VMEM(gn_gamma.shape, F32),
+                pltpu.VMEM(gn_beta.shape, F32),
                 pltpu.VMEM((2, 2, frames, half, chans), BF16),
                 pltpu.VMEM((2, frames + 2, half, 3 * chans), BF16),
                 pltpu.VMEM((2, frames * half, chans), F32),
@@ -517,7 +536,7 @@
                 pltpu.VMEM((8, chans), F32),
                 pltpu.VMEM((2, chans), F32),
                 pltpu.VMEM((2, n_dev, 2, chans), F32),
-                dma((2,)),
+                dma((8,)),
                 dma((2,)),
                 dma((4,)),
                 dma((4,)),
@@ -536,9 +555,9 @@
                 dma((3,)),
                 dma((3,)),
             ],
-            compiler_params=pltpu.CompilerParams(collective_id=0, has_side_effects=True, vmem_limit_bytes=60 * 1024 * 1024),
+            compiler_params=pltpu.CompilerParams(collective_id=0, has_side_effects=True, vmem_limit_bytes=52 * 1024 * 1024),
             name="decode",
-        )(lat, conv_w.reshape(4, 3, 3, 3 * chans, chans), conv_b, gn_gamma, gn_beta)
+        )(*(pltpu.with_memory_space_constraint(a, pltpu.HBM) for a in (lat, conv_w.reshape(4, 3, 3, 3 * chans, chans), conv_b, gn_gamma, gn_beta)))
 
     spec = P(("dp", "cp"), "hp", None, None)
     return jax.shard_map(local_decode, mesh=mesh, in_specs=(spec, P(), P(), P(), P()), out_specs=spec, check_vma=False)

time: 91.5 us -> 89 us (0.973)
  local copies, waits for them, and re-layouts: 2.65 us -> 1.15 us
  Pallas kernels: 88.7 us -> 87.7 us
    unnamed x1, local copies, waits for them, and re-layouts: 2.65 us -> 1.15 us
    pallas_call x1, Pallas kernels: 88.7 us -> 87.7 us  [local_decode(): pl.pallas_call(functools.partial(kernel, (n_cp, frames, half, strip, chan...]
where the time goes in v4:
time: 89 us; the launch traced here: 88.9 us
  Pallas kernels  87.7 us (99%)
  local copies, waits for them, and re-layouts  1.15 us (1%)
    pallas_call x1, Pallas kernels, local_decode(): pl.pallas_call(functools.partial(kernel, (n_cp, frames, half, strip, chan...  87.7 us

profile of v4, /device:TPU:0, one launch (start us, length us, event | category | flops | bytes accessed | tf_op | source)
XLA Modules:
  0.0 88.9 jit_solution(8316107172039854703)
XLA Ops:
  0.0 87.7 %decode.1 = bf16[12,1,128,512]{3,2,1,0:T(8,128)(2,1)S(1)} custom-call(bf16[12,1,128,512]{3,2,1,0:T(8,128)(2,1)} %lat.1, bf16[4,3,3,1536,512]{4,3,2,1,0:T(8,128)(2,1)} %bitcast.1, f32[4,512]{1,0:T(4,128)} %bias_hbm.1, f32[4,512]{1,0:T(4,128)} %gamma_hbm.1, f32[4,512]{1,0:T(4,128)} %beta_hbm.1), custom_call_target="tpu_custom_call" | custom-call | tf_op jit(solution)/shard_map/decode/pallas_call | solution.py:513
  87.7 1.1 %copy.7 = bf16[12,1,128,512]{3,2,1,0:T(8,128)(2,1)} copy(bf16[12,1,128,512]{3,2,1,0:T(8,128)(2,1)S(1)} %decode.1) | data formatting | bytes 3145728

commit v5 on v4

v5 whole, which is shorter than its diff:
```python
import functools

import jax
import jax.numpy as jnp
from jax import lax
from jax.experimental import pallas as pl
from jax.experimental.pallas import tpu as pltpu
from jax.sharding import PartitionSpec as P

GROUPS = 32
EPS = 1e-6
MESH = pl.DeviceIdType.MESH
F32 = jnp.float32
BF16 = jnp.bfloat16
HALVES = OWN, OTH = 0, 1


def kernel(dims, lat, w_hbm, bias_hbm, gamma_hbm, beta_hbm, out, bias, gamma, beta, vid, act, acc, w_buf, x_in, halo, edge, ecol, ext, xact, edge2, ecol2, xres,
           s_acc, s_tot, s_send, s_recv, l_sem, w_sem, xs_sem, xr_sem, hs_sem, hr_sem, es_sem, er_sem, ts_sem, tr_sem, cs_sem, cr_sem,
           rs_sem, ss_sem, sr_sem, o_sem, os_sem, or_sem):
    n_cp, frames, half, strip, chans, count = dims
    n_dev = 2 * n_cp
    per = frames // 4
    h = lax.axis_index("hp")
    r = lax.axis_index("cp")
    me = h * n_cp + r
    partner = {"hp": 1 - h, "cp": r}
    nxt = {"hp": h, "cp": lax.rem(r + 1, n_cp)}
    diag = {"hp": 1 - h, "cp": lax.rem(r + 1, n_cp)}
    not_last = r < n_cp - 1
    not_first = r > 0
    tail = pl.ds(frames - 2, 2)
    my_cols = pl.ds(pl.multiple_of(h * half, half), half)
    ot_cols = pl.ds(pl.multiple_of((1 - h) * half, half), half)
    hc = chans // 2
    lanes = [slice(c * hc, (c + 1) * hc) for c in HALVES]
    part = half - strip
    part_cols = pl.ds(pl.multiple_of(h * strip, strip), part)
    edge_strip = pl.ds(pl.multiple_of((1 - h) * part, strip), strip)

    def remote(src, dst, send, recv, dev):
        return pltpu.make_async_remote_copy(src_ref=src, dst_ref=dst, send_sem=send, recv_sem=recv, device_id=dev, device_id_type=MESH)

    def peer(step):
        t = lax.rem(me + step, n_dev)
        return {"hp": t // n_cp, "cp": lax.rem(t, n_cp)}

    def load_x(k):
        fs = pl.ds(k * per, per)
        return pltpu.make_async_copy(lat.at[fs], x_in.at[fs], l_sem.at[k])

    for k in range(4):
        load_x(k).start()
    small = [pltpu.make_async_copy(a, b, l_sem.at[4 + k]) for k, (a, b) in enumerate([(bias_hbm, bias), (gamma_hbm, gamma), (beta_hbm, beta)])]
    load_own = pltpu.make_async_copy(lat.at[:, 0, my_cols, :], vid.at[0, OWN], l_sem.at[7])

    def w_copy(layer):
        slot = lax.rem(layer, 2)
        return pltpu.make_async_copy(w_hbm.at[layer], w_buf.at[slot], w_sem.at[slot])

    barrier = pltpu.get_barrier_semaphore()
    for step in range(1, n_dev):
        pl.semaphore_signal(barrier, inc=1, device_id=peer(step), device_id_type=MESH)
    for c in small:
        c.start()
    load_own.start()
    w_copy(0).start()

    def fold(v):
        t = v[0:8]
        for k in range(1, v.shape[0] // 8):
            t = t + v[8 * k:8 * k + 8]
        return t

    s_acc[...] = jnp.zeros_like(s_acc)
    s_tot[...] = jnp.zeros_like(s_tot)

    def first_sums(f, carry):
        v = x_in[f, 0].astype(F32)
        for c in HALVES:
            s_acc[c, 0] += fold(v[:, lanes[c]])
            s_acc[c, 1] += fold(v[:, lanes[c]] * v[:, lanes[c]])
        lo, hi = v[half - 1:half], v[half:half + 1]
        ecol[OWN, f] = jnp.where(h == 0, lo, hi)
        edge[0, OWN, f + 2] = jnp.where(h == 0, hi, lo)
        return carry

    for k in range(4):
        load_x(k).wait()
        lax.fori_loop(k * per, (k + 1) * per, first_sums, 0)
    pl.semaphore_wait(barrier, n_dev - 1)

    lane = lax.broadcasted_iota(jnp.int32, (8, hc), 1)
    n_group = chans // GROUPS

    def sum_sends(slot, c):
        return [remote(s_send.at[c], s_recv.at[slot, c, step], ss_sem.at[c, step], sr_sem.at[slot, c, step], peer(step)) for step in range(1, n_dev)]

    def sums_start(slot, c):
        s_send[c, 0:1] = jnp.sum(s_acc[c, 0], axis=0, keepdims=True)
        s_send[c, 1:2] = jnp.sum(s_acc[c, 1], axis=0, keepdims=True)
        s_acc[c] = jnp.zeros_like(s_acc[c])
        for d in sum_sends(slot, c):
            d.start()

    def coefficients(slot, c, layer):
        total = s_send[c]
        for step in range(1, n_dev):
            total = total + s_recv[slot, c, step]
        s_tot[c, 0:2] = total
        t = s_tot[c]
        unit = 1
        while unit < n_group:
            place = (lane // unit) & 3
            g = t
            for d in range(1, 4):
                up = pltpu.roll(t, hc - d * unit, 1)
                down = pltpu.roll(t, (4 - d) * unit, 1)
                g = g + jnp.where(place + d < 4, up, down)
            t = g
            unit *= 4
        t = t * (1.0 / count)
        mean = t[0:1]
        inv = lax.rsqrt(t[1:2] - mean * mean + EPS)
        scale = inv * gamma[pl.ds(layer, 1), lanes[c]]
        return 0.5 * scale, 0.5 * (beta[pl.ds(layer, 1), lanes[c]] - mean * scale)

    def silu(coef, v):
        u = v * coef[0] + coef[1]
        return u + u * jnp.tanh(u)

    def put_shifted(dst, row, p, y, left, right, start):
        n, w = y.shape
        at = lax.broadcasted_iota(jnp.int32, (8, w), 0)
        before = pltpu.roll(y, 1, 0)
        after = pltpu.roll(y, n - 1, 0)
        before = jnp.concatenate([jnp.where(at == 0, left, before[0:8]), before[8:]], axis=0)
        after = jnp.concatenate([after[:n - 8], jnp.where(at == 7, right, after[n - 8:])], axis=0)
        for d, v in enumerate((before, y, after)):
            dst[row, p, :, d * chans + start:d * chans + start + w] = v.astype(BF16)

    def norm(coef, slot, row, p, c):
        v = halo[slot, row, p, :, lanes[c]] if p < 2 else vid[slot, row, p - 2, :, lanes[c]]
        y = silu(coef, v.astype(F32))
        ye = silu(coef, edge[slot, row, p, :, lanes[c]])
        put_shifted(act, row, p, y, jnp.where(h == 0, 0.0, ye), jnp.where(h == 0, ye, 0.0), c * hc)

    def norm_ext(coef, row, p, c):
        mine = silu(coef, (halo[1, row, p, :, lanes[c]] if p < 2 else vid[1, row, p - 2, :, lanes[c]]).astype(F32))
        y = silu(coef, ext[row, p, :, lanes[c]].astype(F32))
        far = silu(coef, edge2[row, p, :, lanes[c]])
        put_shifted(xact, row, p, y, jnp.where(h == 0, mine[half - 1:half], far), jnp.where(h == 0, far, mine[0:1]), c * hc)

    def dots(slot, i, js, lhs, k_half=None, n_half=None):
        cols = slice(0, chans) if n_half is None else lanes[n_half]
        total = None
        for j in js:
            if isinstance(i, int):
                di = 1 if i == j else (2 - 2 * h if i == OWN else 2 * h)
            else:
                di = jnp.where(i == OWN, 1, 2 * h)
            left, right = [], []
            for k in (2, 1, 0):
                for d in range(3):
                    for c in HALVES:
                        if k_half is None or c == k_half:
                            at = slice(d * chans + c * hc, d * chans + (c + 1) * hc)
                            v = lhs(j, k, at)
                            left.append(v.reshape(v.shape[0] * v.shape[1], v.shape[2]))
                            right.append(w_buf[slot, k, di, at, cols])
            q = jnp.dot(jnp.concatenate(left, axis=1), jnp.concatenate(right, axis=0), preferred_element_type=F32)
            total = q if total is None else total + q
        return total

    def frames_of(f0, n):
        return lambda j, k, at: act[j, pl.ds(f0 + k, n), :, at]

    def finish(layer, nslot, i, f0, p, c):
        b = bias[pl.ds(layer, 1), lanes[c]]
        t1 = t2 = None
        for f in range(p.shape[0] // half):
            v = (p[f * half:(f + 1) * half] + b).astype(BF16).astype(F32)
            if isinstance(layer, int):
                vb = v.astype(BF16)
            else:
                res = vid[0, i, f0 + f, :, lanes[c]].astype(F32)
                vb = jnp.where(nslot == 0, res + v, v).astype(BF16)
            vid[nslot, i, f0 + f, :, lanes[c]] = vb
            v = vb.astype(F32)
            t1 = fold(v) if t1 is None else t1 + fold(v)
            t2 = fold(v * v) if t2 is None else t2 + fold(v * v)
            ecol[i, f0 + f, :, lanes[c]] = jnp.where(h == 0, v[half - 1:half], v[0:1])
        s_acc[c, 0] += t1
        s_acc[c, 1] += t2

    def halo_send(slot, row, c):
        return remote(vid.at[slot, row, tail, :, lanes[c]], halo.at[slot, row, :, :, lanes[c]], hs_sem.at[row, c], hr_sem.at[slot, row, c], nxt)

    def edge_send(slot, row, c):
        return remote(ecol.at[row, :, :, lanes[c]], edge.at[slot, 1 - row, pl.ds(2, frames), :, lanes[c]], es_sem.at[row, 0, c],
                      er_sem.at[slot, 1 - row, 0, c], partner)

    def edge_diag(slot, row, c):
        return remote(ecol.at[row, tail, :, lanes[c]], edge.at[slot, 1 - row, pl.ds(0, 2), :, lanes[c]], es_sem.at[row, 1, c],
                      er_sem.at[slot, 1 - row, 1, c], diag)

    def repeat_first(slot, row, cols):
        @pl.when(r == 0)
        def _():
            for f in HALVES:
                halo[slot, row, f, :, cols] = vid[slot, row, 0, :, cols]
                edge[slot, row, f, :, cols] = edge[slot, row, 2, :, cols]

    def half_out(slot, c):
        sums_start(slot, c)
        for row in (OTH, OWN):
            edge_send(slot, row, c).start()

        @pl.when(not_last)
        def _():
            for row in (OTH, OWN):
                edge_diag(slot, row, c).start()
                halo_send(slot, row, c).start()

    def half_in(slot, c, layer):
        for d in sum_sends(slot, c):
            d.wait()
        for row in (OTH, OWN):
            edge_send(slot, row, c).wait()

        @pl.when(not_last)
        def _():
            for row in (OTH, OWN):
                edge_diag(slot, row, c).wait_send()
                halo_send(slot, row, c).wait_send()

        @pl.when(not_first)
        def _():
            for row in (OTH, OWN):
                edge_diag(slot, row, c).wait_recv()
                halo_send(slot, row, c).wait_recv()

        repeat_first(slot, OWN, lanes[c])
        repeat_first(slot, OTH, lanes[c])
        return coefficients(slot, c, layer)

    pieces = [(0, 1), (1, per), (1 + per, per), (1 + 2 * per, frames - 1 - 2 * per)]

    def x_piece(g):
        f0, n = pieces[g]
        return remote(lat.at[pl.ds(f0, n), 0, ot_cols, :], vid.at[0, OTH, pl.ds(f0, n)], xs_sem.at[g], xr_sem.at[g], partner)

    every = slice(0, chans)
    x_halo = remote(lat.at[tail, 0, my_cols, :], halo.at[0, OWN], hs_sem.at[OWN, 0], hr_sem.at[0, OWN, 0], nxt)
    x_pass = remote(vid.at[0, OTH, tail], halo.at[0, OTH], hs_sem.at[OTH, 0], hr_sem.at[0, OTH, 0], nxt)
    e_part = remote(ecol.at[OWN], edge.at[0, OTH, pl.ds(2, frames)], es_sem.at[OWN, 0, 0], er_sem.at[0, OTH, 0, 0], partner)
    e_nxt = remote(edge.at[0, OWN, pl.ds(frames, 2)], edge.at[0, OWN, pl.ds(0, 2)], es_sem.at[OTH, 1, 0], er_sem.at[0, OWN, 1, 0], nxt)
    e_diag = remote(ecol.at[OWN, tail], edge.at[0, OTH, pl.ds(0, 2)], es_sem.at[OWN, 1, 0], er_sem.at[0, OTH, 1, 0], diag)
    for c in HALVES:
        sums_start(0, c)
    e_part.start()

    @pl.when(not_last)
    def _():
        e_diag.start()
        e_nxt.start()
        x_halo.start()

    for g in (3, 2, 1, 0):
        x_piece(g).start()
    w_copy(1).start()
    load_own.wait()
    for c in small:
        c.wait()
    for c in HALVES:
        for d in sum_sends(0, c):
            d.wait()
    coef = [coefficients(0, c, 0) for c in HALVES]
    for p in range(2, frames + 2):
        for c in HALVES:
            norm(coef[c], 0, OWN, p, c)

    @pl.when(not_last)
    def _():
        x_halo.wait_send()
        e_nxt.wait_send()

    @pl.when(not_first)
    def _():
        x_halo.wait_recv()
        e_nxt.wait_recv()

    repeat_first(0, OWN, every)
    for p in range(2):
        for c in HALVES:
            norm(coef[c], 0, OWN, p, c)
    w_copy(0).wait()

    @pl.loop(0, 4)
    def _(c):
        i = c // 2
        f0 = lax.rem(c, 2) * (frames // 2)
        rows = pl.ds(pl.multiple_of(f0 * half, half), frames // 2 * half)
        acc[i, rows, :] = dots(0, i, (OWN,), frames_of(f0, frames // 2))

    e_part.wait()

    @pl.when(not_last)
    def _():
        e_diag.wait_send()

    @pl.when(not_first)
    def _():
        e_diag.wait_recv()

    def last_k(i, g, c):
        rows = pl.ds(g * per * half, per * half)
        finish(0, 1, i, g * per, acc[i, rows, lanes[c]] + dots(0, i, (OTH,), frames_of(g * per, per), n_half=c), c)

    for g in (3, 2, 1, 0):
        x_piece(g).wait()
        if g == 3:
            @pl.when(not_last)
            def _():
                x_pass.start()
        if g == 0:
            @pl.when(not_last)
            def _():
                x_pass.wait_send()

            @pl.when(not_first)
            def _():
                x_pass.wait_recv()

            repeat_first(0, OTH, every)
        for p in reversed(range(g * per, frames + 2 if g == 3 else (g + 1) * per)):
            for c in HALVES:
                norm(coef[c], 0, OTH, p, c)
        rows = pl.ds(g * per * half, per * half)
        for i in (OTH, OWN):
            if g > 1:
                p = acc[i, rows, :] + dots(0, i, (OTH,), frames_of(g * per, per))
                for c in HALVES:
                    finish(0, 1, i, g * per, p[:, lanes[c]], c)
            else:
                last_k(i, g, 0)
    half_out(1, 0)
    for g in (1, 0):
        for i in (OTH, OWN):
            last_k(i, g, 1)
    half_out(1, 1)

    def strip_send(row, c):
        return remote(vid.at[1, row, :, edge_strip, lanes[c]], ext.at[1 - row, pl.ds(2, frames), :, lanes[c]], ts_sem.at[row, 0, c],
                      tr_sem.at[1 - row, 0, c], partner)

    def strip_diag(row, c):
        return remote(vid.at[1, row, tail, edge_strip, lanes[c]], ext.at[1 - row, pl.ds(0, 2), :, lanes[c]], ts_sem.at[row, 1, c],
                      tr_sem.at[1 - row, 1, c], diag)

    def col2_send(row):
        return remote(ecol2.at[row], edge2.at[1 - row, pl.ds(2, frames)], cs_sem.at[row, 0], cr_sem.at[1 - row, 0], partner)

    def col2_diag(row):
        return remote(ecol2.at[row, tail], edge2.at[1 - row, pl.ds(0, 2)], cs_sem.at[row, 1], cr_sem.at[1 - row, 1], diag)

    def res_send():
        return remote(vid.at[0, OTH, :, edge_strip, :], xres, rs_sem.at[0], rs_sem.at[1], partner)

    def layer_body(layer, carry):
        slot = lax.rem(layer, 2)
        nslot = 1 - slot
        w_copy(layer + 1).start()

        @pl.when(layer == 2)
        def _():
            res_send().start()

        def norms(lo, hi, c):
            for row in (OWN, OTH):
                for p in reversed(range(lo, hi)):
                    norm(coef[c], slot, row, p, c)

        def first_k(i, g):
            acc[i, g * per * half:(g + 1) * per * half, :] = dots(slot, i, (OWN, OTH), frames_of(g * per, per), k_half=0)

        coef = [half_in(slot, 0, layer)]
        w_copy(layer).wait()
        norms(3 * per, frames + 2, 0)
        norms(2 * per, 3 * per, 0)
        first_k(OTH, 3)
        norms(per, 2 * per, 0)
        first_k(OTH, 2)
        norms(0, per, 0)
        first_k(OTH, 1)
        first_k(OTH, 0)
        coef.append(half_in(slot, 1, layer))
        norms(3 * per, frames + 2, 1)
        first_k(OWN, 3)
        norms(2 * per, 3 * per, 1)
        first_k(OWN, 2)
        norms(per, 2 * per, 1)
        first_k(OWN, 1)
        norms(0, per, 1)
        first_k(OWN, 0)
        for c in HALVES:
            for i in (OTH, OWN):
                for g in (3, 2, 1, 0):
                    rows = slice(g * per * half, (g + 1) * per * half)
                    p = dots(slot, i, (OWN, OTH), frames_of(g * per, per), k_half=1, n_half=c)
                    finish(layer, nslot, i, g * per, acc[i, rows, lanes[c]] + p, c)
            half_out(nslot, c)

            @pl.when(layer == 2)
            def _():
                for row in (OTH, OWN):
                    strip_send(row, c).start()

                @pl.when(not_last)
                def _():
                    for row in (OTH, OWN):
                        strip_diag(row, c).start()

        return carry

    lax.fori_loop(1, 3, layer_body, 0)

    wide = frames // 4
    pieces_out = (3, 2, 1, 0)

    def out_send(k):
        fs = pl.ds(k * wide, wide)
        dst = out.at[fs, 0, pl.ds(pl.multiple_of(h * (half + strip), strip), part), :]
        return remote(vid.at[0, OTH, fs, part_cols, :], dst, os_sem.at[k], or_sem.at[k], partner)

    def out_local():
        return pltpu.make_async_copy(vid.at[0, OWN], out.at[:, 0, my_cols, :], o_sem.at[0])

    def out_ext():
        dst = out.at[:, 0, pl.ds(pl.multiple_of(half - h * strip, strip), strip), :]
        return pltpu.make_async_copy(xres, dst, o_sem.at[1])

    def norms(lo, hi, c):
        for row in (OWN, OTH):
            for p in reversed(range(lo, hi)):
                norm(coef[c], 1, row, p, c)

    def close(res, p):
        return (res.astype(F32) + (p + bias[3:4, :]).astype(BF16).astype(F32)).astype(BF16)

    def part_dots(k, k_half):
        return dots(1, OTH, (OWN, OTH), lambda j, t, at: act[j, pl.ds(k * wide + t, wide), part_cols, at], k_half)

    def part_chunk(k):
        rows = slice(k * wide * part, (k + 1) * wide * part)
        p = acc[OTH, rows, :] + part_dots(k, 1)
        for f in range(wide):
            fr = k * wide + f
            vid[0, OTH, fr, part_cols, :] = close(vid[0, OTH, fr, part_cols, :], p[f * part:(f + 1) * part])
        out_send(k).start()

    def own_chunk(g):
        if g == 3:
            p = acc[OWN, g * per * half:(g + 1) * per * half, :] + dots(1, OWN, (OWN, OTH), frames_of(g * per, per), 1)
        else:
            p = dots(1, OWN, (OWN, OTH), frames_of(g * per, per))
        for f in range(per):
            vid[0, OWN, g * per + f] = close(vid[0, OWN, g * per + f], p[f * half:(f + 1) * half])

    coef = [half_in(1, 0, 3)]
    w_copy(3).wait()
    def norms_for(k, c):
        norms(k * wide, frames + 2 if k == 3 else (k + 1) * wide, c)

    norms_for(3, 0)
    norms_for(2, 0)
    for k in pieces_out:
        acc[OTH, k * wide * part:(k + 1) * wide * part, :] = part_dots(k, 0)
        if k > 1:
            norms_for(k - 2, 0)
    acc[OWN, 3 * per * half:4 * per * half, :] = dots(1, OWN, (OWN, OTH), frames_of(3 * per, per), 0)

    def columns2(f, carry):
        for row in (OWN, OTH):
            v = vid[1, row, f, strip:half - strip, :].astype(F32)
            ecol2[row, f] = jnp.where(h == 0, v[half - 2 * strip - 1:half - 2 * strip], v[0:1])
        return carry

    lax.fori_loop(0, frames, columns2, 0)
    for row in (OWN, OTH):
        col2_send(row).start()

    @pl.when(not_last)
    def _():
        for row in (OWN, OTH):
            col2_diag(row).start()

    coef.append(half_in(1, 1, 3))
    norms_for(3, 1)
    for k in pieces_out:
        if k > 0:
            norms_for(k - 1, 1)
        part_chunk(k)
    for row in (OWN, OTH):
        col2_send(row).wait()
        for c in HALVES:
            strip_send(row, c).wait()

    @pl.when(not_last)
    def _():
        for row in (OWN, OTH):
            col2_diag(row).wait_send()
            for c in HALVES:
                strip_diag(row, c).wait_send()

    @pl.when(not_first)
    def _():
        for row in (OWN, OTH):
            col2_diag(row).wait_recv()
            for c in HALVES:
                strip_diag(row, c).wait_recv()

    @pl.when(r == 0)
    def _():
        for row in (OWN, OTH):
            for f in HALVES:
                ext[row, f] = ext[row, 2]
                edge2[row, f] = edge2[row, 2]

    res_send().wait()
    for row in (OWN, OTH):
        for p in range(frames + 2):
            for c in HALVES:
                norm_ext(coef[c], row, p, c)
    for g in (3, 2, 1, 0):
        own_chunk(g)
    p = dots(1, OWN, (OWN, OTH), lambda j, t, at: xact[j, pl.ds(t, frames), :, at])
    out_local().start()
    for f in range(frames):
        xres[f] = close(xres[f], p[f * strip:(f + 1) * strip])
    out_ext().start()
    out_local().wait()
    out_ext().wait()
    for k in pieces_out:
        out_send(k).wait()


def solution(mesh):
    n_cp = mesh.shape["cp"]

    def local_decode(lat, conv_w, conv_b, gn_gamma, gn_beta):
        frames, _, width, chans = lat.shape
        half = width // 2
        strip = half // 4
        n_dev = 2 * n_cp
        count = frames * n_cp * 2 * width * (chans // GROUPS)
        dma = pltpu.SemaphoreType.DMA

        def pair(*more):
            return dma((2, *more))

        any_spec = pl.BlockSpec(memory_space=pl.ANY)
        return pl.pallas_call(
            functools.partial(kernel, (n_cp, frames, half, strip, chans, count)),
            out_shape=jax.ShapeDtypeStruct(lat.shape, BF16),
            in_specs=[any_spec] * 5,
            out_specs=any_spec,
            scratch_shapes=[
                pltpu.VMEM(conv_b.shape, F32),
                pltpu.VMEM(gn_gamma.shape, F32),
                pltpu.VMEM(gn_beta.shape, F32),
                pltpu.VMEM((2, 2, frames, half, chans), BF16),
                pltpu.VMEM((2, frames + 2, half, 3 * chans), BF16),
                pltpu.VMEM((2, frames * half, chans), F32),
                pltpu.VMEM((2, 3, 3, 3 * chans, chans), BF16),
                pltpu.VMEM(lat.shape, BF16),
                pltpu.VMEM((2, 2, 2, half, chans), BF16),
                pltpu.VMEM((2, 2, frames + 2, 1, chans), F32),
                pltpu.VMEM((2, frames, 1, chans), F32),
                pltpu.VMEM((2, frames + 2, strip, chans), BF16),
                pltpu.VMEM((2, frames + 2, strip, 3 * chans), BF16),
                pltpu.VMEM((2, frames + 2, 1, chans), F32),
                pltpu.VMEM((2, frames, 1, chans), F32),
                pltpu.VMEM((frames, strip, chans), BF16),
                pltpu.VMEM((2, 2, 8, chans // 2), F32),
                pltpu.VMEM((2, 8, chans // 2), F32),
                pltpu.VMEM((2, 2, chans // 2), F32),
                pltpu.VMEM((2, 2, n_dev, 2, chans // 2), F32),
                dma((8,)),
                pair(),
                dma((4,)),
                dma((4,)),
                pair(2),
                pair(2, 2),
                pair(2, 2),
                pair(2, 2, 2),
                pair(2, 2),
                pair(2, 2),
                pair(2),
                pair(2),
                pair(),
                pair(n_dev),
                pair(2, n_dev),
                pair(),
                dma((4,)),
                dma((4,)),
            ],
            compiler_params=pltpu.CompilerParams(collective_id=0, has_side_effects=True, vmem_limit_bytes=52 * 1024 * 1024),
            name="decode",
        )(*(pltpu.with_memory_space_constraint(a, pltpu.HBM) for a in (lat, conv_w.reshape(4, 3, 3, 3 * chans, chans), conv_b, gn_gamma, gn_beta)))

    spec = P(("dp", "cp"), "hp", None, None)
    return jax.shard_map(local_decode, mesh=mesh, in_specs=(spec, P(), P(), P(), P()), out_specs=spec, check_vma=False)
```

time: 89 us -> 85.7 us (0.963)
  Pallas kernels: 87.7 us -> 84.4 us
    pallas_call x1, Pallas kernels: 87.7 us -> 84.4 us  [local_decode(): pl.pallas_call(functools.partial(kernel, (n_cp, frames, half, strip, chan...]
where the time goes in v5:
time: 85.7 us; the launch traced here: 85.6 us
  Pallas kernels  84.4 us (98%)
  local copies, waits for them, and re-layouts  1.15 us (1%)
    pallas_call x1, Pallas kernels, local_decode(): pl.pallas_call(functools.partial(kernel, (n_cp, frames, half, strip, chan...  84.4 us

profile of v5, /device:TPU:0, one launch (start us, length us, event | category | flops | bytes accessed | tf_op | source)
XLA Modules:
  0.0 85.6 jit_solution(16473303502613234323)
XLA Ops:
  0.0 84.4 %decode.1 = bf16[12,1,128,512]{3,2,1,0:T(8,128)(2,1)S(1)} custom-call(bf16[12,1,128,512]{3,2,1,0:T(8,128)(2,1)} %lat.1, bf16[4,3,3,1536,512]{4,3,2,1,0:T(8,128)(2,1)} %bitcast.1, f32[4,512]{1,0:T(4,128)} %bias_hbm.1, f32[4,512]{1,0:T(4,128)} %gamma_hbm.1, f32[4,512]{1,0:T(4,128)} %beta_hbm.1), custom_call_target="tpu_custom_call" | custom-call | tf_op jit(solution)/shard_map/decode/pallas_call | solution.py:563
  84.4 1.1 %copy.7 = bf16[12,1,128,512]{3,2,1,0:T(8,128)(2,1)} copy(bf16[12,1,128,512]{3,2,1,0:T(8,128)(2,1)S(1)} %decode.1) | data formatting | bytes 3145728

commit v6 on v5

--- a/solution.py
+++ b/solution.py
@@ -85,10 +85,18 @@
         edge[0, OWN, f + 2] = jnp.where(h == 0, hi, lo)
         return carry
 
+    starts = (0, 1, 1 + per, 1 + 2 * per, frames - 1, frames)
+
+    def x_piece(g):
+        fs = pl.ds(starts[g], starts[g + 1] - starts[g])
+        return remote(lat.at[fs, 0, ot_cols, :], vid.at[0, OTH, fs], xs_sem.at[g], xr_sem.at[g], partner)
+
     for k in range(4):
         load_x(k).wait()
+        if k == 1:
+            pl.semaphore_wait(barrier, n_dev - 1)
+            x_piece(4).start()
         lax.fori_loop(k * per, (k + 1) * per, first_sums, 0)
-    pl.semaphore_wait(barrier, n_dev - 1)
 
     lane = lax.broadcasted_iota(jnp.int32, (8, hc), 1)
     n_group = chans // GROUPS
@@ -160,7 +168,7 @@
             else:
                 di = jnp.where(i == OWN, 1, 2 * h)
             left, right = [], []
-            for k in (2, 1, 0):
+            for k in reversed(range(3)):
                 for d in range(3):
                     for c in HALVES:
                         if k_half is None or c == k_half:
@@ -244,12 +252,6 @@
         repeat_first(slot, OTH, lanes[c])
         return coefficients(slot, c, layer)
 
-    pieces = [(0, 1), (1, per), (1 + per, per), (1 + 2 * per, frames - 1 - 2 * per)]
-
-    def x_piece(g):
-        f0, n = pieces[g]
-        return remote(lat.at[pl.ds(f0, n), 0, ot_cols, :], vid.at[0, OTH, pl.ds(f0, n)], xs_sem.at[g], xr_sem.at[g], partner)
-
     every = slice(0, chans)
     x_halo = remote(lat.at[tail, 0, my_cols, :], halo.at[0, OWN], hs_sem.at[OWN, 0], hr_sem.at[0, OWN, 0], nxt)
     x_pass = remote(vid.at[0, OTH, tail], halo.at[0, OTH], hs_sem.at[OTH, 0], hr_sem.at[0, OTH, 0], nxt)
@@ -320,6 +322,8 @@
     for g in (3, 2, 1, 0):
         x_piece(g).wait()
         if g == 3:
+            x_piece(4).wait()
+
             @pl.when(not_last)
             def _():
                 x_pass.start()
@@ -588,8 +592,8 @@
                 pltpu.VMEM((2, 2, n_dev, 2, chans // 2), F32),
                 dma((8,)),
                 pair(),
-                dma((4,)),
-                dma((4,)),
+                dma((5,)),
+                dma((5,)),
                 pair(2),
                 pair(2, 2),
                 pair(2, 2),

time: 85.7 us -> 85.3 us (level)
  no operation moved by 1% of the time
where the time goes in v6:
time: 85.3 us; the launch traced here: 85.2 us
  Pallas kernels  84.1 us (99%)
  local copies, waits for them, and re-layouts  1.15 us (1%)
    pallas_call x1, Pallas kernels, local_decode(): pl.pallas_call(functools.partial(kernel, (n_cp, frames, half, strip, chan...  84.1 us

profile of v6, /device:TPU:0, one launch (start us, length us, event | category | flops | bytes accessed | tf_op | source)
XLA Modules:
  0.0 85.2 jit_solution(4251925731447002101)
XLA Ops:
  0.0 84.1 %decode.1 = bf16[12,1,128,512]{3,2,1,0:T(8,128)(2,1)S(1)} custom-call(bf16[12,1,128,512]{3,2,1,0:T(8,128)(2,1)} %lat.1, bf16[4,3,3,1536,512]{4,3,2,1,0:T(8,128)(2,1)} %bitcast.1, f32[4,512]{1,0:T(4,128)} %bias_hbm.1, f32[4,512]{1,0:T(4,128)} %gamma_hbm.1, f32[4,512]{1,0:T(4,128)} %beta_hbm.1), custom_call_target="tpu_custom_call" | custom-call | tf_op jit(solution)/shard_map/decode/pallas_call | solution.py:567
  84.1 1.1 %copy.7 = bf16[12,1,128,512]{3,2,1,0:T(8,128)(2,1)} copy(bf16[12,1,128,512]{3,2,1,0:T(8,128)(2,1)S(1)} %decode.1) | data formatting | bytes 3145728
